TPU v7x, 32 devices: a whole 2x2x4 slice. The times are simulated.
32 devices in a mesh: trial: 2 (over x), shard: 4 (over y, core), cols: 4 (over z).
Axes of the slice: x: 2, y: 2, z: 4, core: 2. Of those that a mesh axis runs over, the one named last changes fastest.
Arguments:
- train_gate: bfloat16 [4096, 8192], P(('trial', 'shard'), 'cols'), parts along dimension 0, may hold values from -0.125 to 0.125
- low_gate: bfloat16 [4096, 16], P(('trial', 'shard')), parts along dimension 0, may hold values from -0.125 to 0.125
- high_gate: bfloat16 [32, 8192], P('trial', 'cols'), parts along dimension 0, may hold values from -1.5 to 1.5
- train_up: bfloat16 [4096, 8192], P(('trial', 'shard'), 'cols'), parts along dimension 0, may hold values from -0.125 to 0.125
- low_up: bfloat16 [4096, 16], P(('trial', 'shard')), parts along dimension 0, may hold values from -0.125 to 0.125
- high_up: bfloat16 [32, 8192], P('trial', 'cols'), parts along dimension 0, may hold values from -1.5 to 1.5
- norm_train: float32 [4096], P(('trial', 'shard', 'cols')), parts along dimension 0, may hold values from 0.25 to 1.75
- norm_step: float32 [4096], P(('trial', 'shard', 'cols')), parts along dimension 0, may hold values from -0.3 to 0.3
Outputs:
- serve_gate: bfloat16 [16384, 2048], P(('trial', 'cols')), parts along dimension 0
- serve_up: bfloat16 [16384, 2048], P(('trial', 'cols')), parts along dimension 0
- serve_norm: bfloat16 [4096], P('trial'), parts along dimension 0
There are 2 independent parts, one for each index of `trial`. A program takes and returns all parts, laid end to end along the dimension named above; each array names one. Nothing has to cross between parts.
All inputs are finite; a program needn't handle non-finite values.
Results may differ from a plain program's by a relative error of at most 0.001.
Values may be sent and summed in bfloat16 or wider, within the bound.
A program may use at most 128 MiB of HBM per device.

v0:
```python
import jax
import jax.numpy as jnp
from jax import lax
from jax.sharding import PartitionSpec as P

mix_rate = 2.0


def local(train_gate, low_gate, high_gate, train_up, low_up, high_up, norm_train, norm_step):
    fresh_gate = train_gate.astype(jnp.float32) + mix_rate * jnp.dot(
        low_gate, high_gate, preferred_element_type=jnp.float32
    )
    fresh_up = train_up.astype(jnp.float32) + mix_rate * jnp.dot(
        low_up, high_up, preferred_element_type=jnp.float32
    )
    narrow_gate, narrow_up = (fresh_gate.astype(jnp.bfloat16), fresh_up.astype(jnp.bfloat16))
    serve_gate, serve_up = (
        lax.all_gather(narrow_gate, "shard", axis=0, tiled=True),
        lax.all_gather(narrow_up, "shard", axis=0, tiled=True),
    )
    serve_gate, serve_up = (serve_gate.T, serve_up.T)
    serve_norm = lax.all_gather(
        (norm_train + norm_step).astype(jnp.bfloat16), ("shard", "cols"), axis=0, tiled=True
    )
    return (serve_gate, serve_up, serve_norm)


def solution(mesh):
    return jax.shard_map(
        local,
        mesh=mesh,
        in_specs=(
            P(("trial", "shard"), "cols"),
            P(("trial", "shard"), None),
            P("trial", "cols"),
            P(("trial", "shard"), "cols"),
            P(("trial", "shard"), None),
            P("trial", "cols"),
            P(("trial", "shard", "cols")),
            P(("trial", "shard", "cols")),
        ),
        out_specs=(P(("trial", "cols"), None), P(("trial", "cols"), None), P("trial")),
        check_vma=False,
    )
```

profile of v0, /device:TPU:0, one launch (start us, length us, event | category | flops | bytes accessed | tf_op | source)
XLA Modules:
  0.0 151.8 jit_solution(14837841643282146696)
XLA Ops:
  7.2 0.0 copy-start
  7.2 0.0 copy-start.1
  7.2 0.0 copy-start.3
  7.2 0.0 copy-start.2
  7.2 0.0 all-gather.4.cloned.1.call-start
  7.3 0.8 copy-done
  8.0 3.7 %add_convert_fusion.1 = bf16[512,2048]{1,0:T(8,128)(2,1)} fusion(bf16[512,2048]{1,0:T(8,128)(2,1)} %param.8, bf16[512,16]{0,1:T(8,128)(2,1)} %param.9, bf16[16,2048]{1,0:T(8,128)(2,1)S(1)} %copy-done), kind=kOutput, calls=%fused_computation.1 | convolution fusion | flops 37748736 | bytes 4276224 | tf_op jit(solution)/shard_map/dot_general | solution.py:10
  11.7 0.0 copy-start.4
  11.7 0.0 copy-start.5
  11.7 0.0 all-gather.4.cloned.1.call-update
  11.7 0.0 all-gather.6.cloned.1.call-start
  11.7 0.0 copy-done.1
  11.8 0.0 copy-done.3
  11.8 0.0 copy-done.2
  11.8 2.1 %add_convert_fusion = bf16[512,2048]{1,0:T(8,128)(2,1)} fusion(bf16[512,2048]{1,0:T(8,128)(2,1)S(1)} %copy-done.1, bf16[512,16]{0,1:T(8,128)(2,1)S(1)} %copy-done.3, bf16[16,2048]{1,0:T(8,128)(2,1)S(1)} %copy-done.2), kind=kOutput, calls=%fused_computation | convolution fusion | flops 37748736 | bytes 4276224 | tf_op jit(solution)/shard_map/dot_general | solution.py:13
  13.8 0.0 all-gather.6.cloned.1.call-update
  13.9 0.0 copy-done.4
  13.9 0.0 copy-done.5
  13.9 33.9 %all-gather = bf16[16,1,128]{2,1,0:T(2,128)(2,1)S(1)} all-gather(bf16[1,1,128]{2,1,0:T(2,128)(2,1)S(1)} %convert_bitcast_fusion), channel_id=1, replica_groups=mesh['trial'=2,'shard'=4,'cols'=4] {'shard','cols'}, dimensions={0}, use_global_device_ids=true | all-gather | bytes 4352 | tf_op jit(solution)/shard_map/all_gather | solution.py:22
  47.8 0.6 reduce
  48.5 24.4 %all-gather.4.cloned.1.call-done = bf16[2048,2048]{1,0:T(8,128)(2,1)} async-done(((bf16[512,2048]{1,0:T(8,128)(2,1)}), bf16[2048,2048]{1,0:T(8,128)(2,1)}) %all-gather.4.cloned.1.call-update) | async-done | bytes 8388624 | tf_op jit(solution)/shard_map/all_gather | solution.py:18
  72.9 12.4 %copy.15 = bf16[2048,2048]{1,0:T(8,128)(2,1)} copy(bf16[2048,2048]{0,1:T(8,128)(2,1)} %bitcast.9) | data formatting | bytes 16777216
  85.2 47.5 %all-gather.6.cloned.1.call-done = bf16[2048,2048]{1,0:T(8,128)(2,1)} async-done(((bf16[512,2048]{1,0:T(8,128)(2,1)}), bf16[2048,2048]{1,0:T(8,128)(2,1)}) %all-gather.6.cloned.1.call-update) | async-done | bytes 8388624 | tf_op jit(solution)/shard_map/all_gather | solution.py:19
  132.7 12.2 %copy.16 = bf16[2048,2048]{1,0:T(8,128)(2,1)} copy(bf16[2048,2048]{0,1:T(8,128)(2,1)} %bitcast.10) | data formatting | bytes 16777216
  (1 shorter events, 0.0 us)
Async XLA Ops:
  7.2 0.8 copy-start
  7.2 4.6 %copy-start.1 = (bf16[512,2048]{1,0:T(8,128)(2,1)S(1)}, bf16[512,2048]{1,0:T(8,128)(2,1)}, u32[]{:S(2)}) copy-start(bf16[512,2048]{1,0:T(8,128)(2,1)} %param.11) | copy-start | bytes 6291460
  7.2 4.6 %copy-start.3 = (bf16[512,16]{0,1:T(8,128)(2,1)S(1)}, bf16[512,16]{0,1:T(8,128)(2,1)}, u32[]{:S(2)}) copy-start(bf16[512,16]{0,1:T(8,128)(2,1)} %param.12) | copy-start | bytes 49156
  7.2 4.6 %copy-start.2 = (bf16[16,2048]{1,0:T(8,128)(2,1)S(1)}, bf16[16,2048]{1,0:T(8,128)(2,1)}, u32[]{:S(2)}) copy-start(bf16[16,2048]{1,0:T(8,128)(2,1)} %param.13) | copy-start | bytes 196612
  7.2 65.7 %all-gather.4.cloned.1.call-start = ((), (), s32[]{:S(2)}) async-start(), calls=%async_computation | async-start | bytes 10485760 | tf_op jit(solution)/shard_map/all_gather | solution.py:18
  11.7 2.2 %copy-start.4 = (f32[128]{0:T(128)S(1)}, f32[128]{0:T(128)}, u32[]{:S(2)}) copy-start(f32[128]{0:T(128)} %param.14) | copy-start | bytes 1540
  11.7 2.2 %copy-start.5 = (f32[128]{0:T(128)S(1)}, f32[128]{0:T(128)}, u32[]{:S(2)}) copy-start(f32[128]{0:T(128)} %param.15) | copy-start | bytes 1540
  11.7 121.0 %all-gather.6.cloned.1.call-start = ((), (), s32[]{:S(2)}) async-start(), calls=%async_computation.1 | async-start | bytes 10485760 | tf_op jit(solution)/shard_map/all_gather | solution.py:19
Sparse Core Ops, SparseCore 0:
  11.8 61.0 all-gather.3
  74.4 58.2 all-gather.5
where the time goes:
time: 153 us; the launch traced here: 152 us
  waiting for transfers between devices  71.9 us (47%)
  blocking collectives  33.9 us (22%)
  local copies, waits for them, and re-layouts  25.4 us (17%)
  between operations  14.1 us (9%)
  matrix products  5.72 us (4%)
    all_gather x1, waiting for transfers between devices, local(): lax.all_gather(narrow_up, 'shard', axis=0, tiled=True)  47.5 us
    all_gather x1, blocking collectives, local(): lax.all_gather((norm_train + norm_step).astype(jnp.bfloat16), ('shard', '...  33.9 us
    unnamed x14, local copies, waits for them, and re-layouts  25.4 us
    all_gather x1, waiting for transfers between devices, local(): lax.all_gather(narrow_gate, 'shard', axis=0, tiled=True)  24.4 us
    dot_general x1, matrix products, local(): jnp.dot(low_gate, high_gate, preferred_element_type=jnp.float32)  3.66 us
  transfers between devices with their start and end apart: 2, of which 2 were waited for; matrix products, arithmetic and copies ran while one was open for 10% of the time, Pallas kernels for 0%

commit v1 on v0

v1 whole, which is shorter than its diff:
```python
import functools

import jax
import jax.numpy as jnp
from jax import lax
from jax.experimental import pallas as pl
from jax.experimental.pallas import tpu as pltpu
from jax.sharding import PartitionSpec as P


mix_rate = 2.0
ANY = pl.BlockSpec(memory_space=pl.ANY)
TILE = 256
PIECES = ((1, 2, 2, 3), (3, 2, 2, 1))
UNITS = 8


def merge_kernel(train_ref, low_ref, high_ref, out_ref):
    change = lax.dot_general(
        low_ref[...],
        high_ref[...],
        (((0,), (0,)), ((), ())),
        preferred_element_type=jnp.float32,
    )
    fresh = train_ref[...].astype(jnp.float32) + mix_rate * change
    out_ref[...] = fresh.astype(jnp.bfloat16).T


def merge(train, low, high, first, size):
    rank, rows = low.shape
    tile = TILE
    skip = first // tile
    return pl.pallas_call(
        merge_kernel,
        grid=(size // tile,),
        in_specs=[
            pl.BlockSpec((rows, tile), lambda i: (0, i + skip)),
            pl.BlockSpec((rank, rows), lambda i: (0, 0)),
            pl.BlockSpec((rank, tile), lambda i: (0, i + skip)),
        ],
        out_specs=pl.BlockSpec((tile, rows), lambda i: (i, 0)),
        out_shape=jax.ShapeDtypeStruct((size, rows), jnp.bfloat16),
        cost_estimate=pl.CostEstimate(
            flops=2 * size * rows * rank, bytes_accessed=4 * size * rows, transcendentals=0
        ),
    )(train, low, high)


def place_kernel(masks, first, started, *refs):
    blocks = refs[: len(masks)]
    out_ref, held, in_sem, out_sem = refs[len(masks) + (1 if started else 0) :]
    size, width = blocks[0].shape
    me = lax.axis_index("shard")
    loads, stores = [], []
    for j, block in enumerate(blocks):
        load = pltpu.make_async_copy(block, held.at[j], in_sem.at[j])
        load.start()
        loads.append(load)
    for j, mask in enumerate(masks):
        loads[j].wait()
        column = pl.multiple_of((me ^ mask) * width, width)
        store = pltpu.make_async_copy(
            held.at[j],
            out_ref.at[pl.ds(first, size), pl.ds(column, width)],
            out_sem.at[j],
        )
        store.start()
        stores.append(store)
    for store in stores:
        store.wait()


def place(whole, shape, blocks, masks, first):
    started = whole is not None
    count = len(blocks)
    return pl.pallas_call(
        functools.partial(place_kernel, masks, first, started),
        in_specs=[ANY] * (count + started),
        out_specs=ANY,
        out_shape=jax.ShapeDtypeStruct(shape, jnp.bfloat16),
        scratch_shapes=[
            pltpu.VMEM((count,) + blocks[0].shape, jnp.bfloat16),
            pltpu.SemaphoreType.DMA((count,)),
            pltpu.SemaphoreType.DMA((count,)),
        ],
        input_output_aliases={count: 0} if started else {},
        cost_estimate=pl.CostEstimate(
            flops=0, bytes_accessed=4 * count * blocks[0].size, transcendentals=0
        ),
    )(*blocks, *([whole] if started else []))


def swap(x, axis, size, bit):
    return lax.ppermute(x, axis, [(i, i ^ bit) for i in range(size)])


def cuts(inner):
    found = []
    for which, units in enumerate(PIECES):
        first = 0
        for unit in units:
            found.append((which, first, unit * inner // UNITS))
            first += found[-1][2]
    return found


def gathered(n, pairs):
    rows, inner = pairs[0][0].shape
    queue = []
    for which, first, size in cuts(inner):
        train, low, high = pairs[which]
        own = merge(train, low.T, high, first, size)
        queue.append((which, first, [own, swap(own, "shard", n, n // 2)], [0, n // 2]))
    whole, last = [None] * len(pairs), None
    for which, first, held, masks in queue:
        if last is not None:
            whole[last], held[1] = lax.optimization_barrier((whole[last], held[1]))
        bit = n // 4
        while bit:
            held = held + [swap(h, "shard", n, bit) for h in held]
            masks = masks + [m ^ bit for m in masks]
            bit //= 2
        whole[which] = place(whole[which], (inner, n * rows), held, tuple(masks), first)
        last = which
    return whole


def norm_gathered(n, m, gain):
    me = lax.axis_index("shard") * m + lax.axis_index("cols")
    held = jnp.where(jnp.arange(n * m)[:, None] == me, gain[None, :], jnp.zeros((), gain.dtype))
    for axis, size in (("cols", m), ("shard", n)):
        bit = 1
        while bit < size:
            held = held + swap(held, axis, size, bit)
            bit *= 2
    return held.reshape(-1)


def plain(train, low, high):
    fresh = train.astype(jnp.float32) + mix_rate * jnp.dot(
        low, high, preferred_element_type=jnp.float32
    )
    return lax.all_gather(fresh.astype(jnp.bfloat16), "shard", axis=0, tiled=True).T


def power(n):
    return n & (n - 1) == 0


def fits(n, m, rows, inner):
    return n > 1 and power(n) and power(m) and rows % 128 == 0 and inner % (TILE * UNITS) == 0


def local(n, m, train_gate, low_gate, high_gate, train_up, low_up, high_up, norm_train, norm_step):
    pairs = [(train_gate, low_gate, high_gate), (train_up, low_up, high_up)]
    gain = (norm_train + norm_step).astype(jnp.bfloat16)
    if not fits(n, m, *train_gate.shape):
        serve_gate, serve_up = [plain(*pair) for pair in pairs]
        serve_norm = lax.all_gather(gain, ("shard", "cols"), axis=0, tiled=True)
        return serve_gate, serve_up, serve_norm
    serve_norm = norm_gathered(n, m, gain)
    serve_gate, serve_up = gathered(n, pairs)
    return serve_gate, serve_up, serve_norm


def solution(mesh):
    n, m = mesh.shape["shard"], mesh.shape["cols"]
    return jax.shard_map(
        functools.partial(local, n, m),
        mesh=mesh,
        in_specs=(
            P(("trial", "shard"), "cols"),
            P(("trial", "shard"), None),
            P("trial", "cols"),
            P(("trial", "shard"), "cols"),
            P(("trial", "shard"), None),
            P("trial", "cols"),
            P(("trial", "shard", "cols")),
            P(("trial", "shard", "cols")),
        ),
        out_specs=(P(("trial", "cols"), None), P(("trial", "cols"), None), P("trial")),
        check_vma=False,
    )
```

time: 153 us -> 136 us (0.89)
  Pallas kernels: 0 us -> 40 us
  blocking collectives: 33.9 us -> 0 us
  starting transfers between devices: 0.08 us -> 18.6 us
  local copies, waits for them, and re-layouts: 25.4 us -> 8.71 us
  between operations: 14.1 us -> 0.87 us
  matrix products: 5.72 us -> 0 us
  waiting for transfers between devices: 71.9 us -> 66.2 us
    all_gather x2 -> x0, waiting for transfers between devices: 71.9 us -> none  [the longest x1 47.5 us: local(): lax.all_gather(narrow_up, 'shard', axis=0, tiled=True)]
    ppermute x0 -> x28, waiting for transfers between devices: none -> 66.2 us  [swap(): return lax.ppermute(x, axis, [(i, i ^ bit) for i in range(size)])]
    pallas_call x0 -> x16, Pallas kernels: none -> 40 us  [the longest x8 20.6 us: merge(): pl.pallas_call(merge_kernel, grid=(size // tile,), in_specs=[pl.BlockSpec...]
    all_gather x1 -> x0, blocking collectives: 33.9 us -> none  [local(): lax.all_gather((norm_train + norm_step).astype(jnp.bfloat16), ('shard', '...]
    ppermute x0 -> x28, starting transfers between devices: none -> 18.6 us  [swap(): return lax.ppermute(x, axis, [(i, i ^ bit) for i in range(size)])]
    unnamed x14 -> x46, local copies, waits for them, and re-layouts: 25.4 us -> 8.71 us
    dot_general x2 -> x0, matrix products: 5.72 us -> none  [the longest x1 3.66 us: local(): jnp.dot(low_gate, high_gate, preferred_element_type=jnp.float32)]
  transfers between devices with their start and end apart: 2 -> 28, of which waited for: 2 -> 12; matrix products, arithmetic and copies ran while one was open for 10% -> 1% of each run, Pallas kernels for 0% -> 27%
where the time goes in v1:
time: 136 us; the launch traced here: 135 us
  waiting for transfers between devices  66.2 us (49%)
  Pallas kernels  40 us (29%)
  starting transfers between devices  18.6 us (14%)
  local copies, waits for them, and re-layouts  8.71 us (6%)
    ppermute x28, waiting for transfers between devices, swap(): return lax.ppermute(x, axis, [(i, i ^ bit) for i in range(size)])  66.2 us
    pallas_call x8, Pallas kernels, merge(): pl.pallas_call(merge_kernel, grid=(size // tile,), in_specs=[pl.BlockSpec...  20.6 us
    pallas_call x8, Pallas kernels, place(): pl.pallas_call(functools.partial(place_kernel, masks, first, started), in...  19.3 us
    ppermute x28, starting transfers between devices, swap(): return lax.ppermute(x, axis, [(i, i ^ bit) for i in range(size)])  18.6 us
    unnamed x46, local copies, waits for them, and re-layouts  8.71 us
  transfers between devices with their start and end apart: 28, of which 12 were waited for; matrix products, arithmetic and copies ran while one was open for 1% of the time, Pallas kernels for 27%

profile of v1, /device:TPU:0, one launch (start us, length us, event | category | flops | bytes accessed | tf_op | source)
XLA Modules:
  0.0 135.2 jit_solution(1259573531023520220)
XLA Ops:
  0.6 2.0 %shard_map.106.refs_0_ = bf16[256,512]{1,0:T(8,128)(2,1)} custom-call(bf16[512,2048]{1,0:T(8,128)(2,1)} %train_ref.11, bf16[16,512]{1,0:T(8,128)(2,1)} %bitcast.4, bf16[16,2048]{1,0:T(8,128)(2,1)} %high_ref.11), custom_call_target="tpu_custom_call" | custom-call | flops 4194304 | bytes 524288 | tf_op jit(solution)/shard_map/pallas_call | solution.py:33
  2.6 3.0 %collective-permute-start = (bf16[256,512]{1,0:T(8,128)(2,1)}, bf16[256,512]{1,0:T(8,128)(2,1)S(1)}, u32[]{:S(2)}, u32[]{:S(2)}) collective-permute-start(bf16[256,512]{1,0:T(8,128)(2,1)} %shard_map.106.refs_0_), channel_id=1, source_target_pairs={{0,8},{4,12},{8,0},{12,4},{1,9},{5,13},{9,1},{13,5},{2,10},{6,14},... | collective-permute-start | bytes 786440 | tf_op jit(solution)/shard_map/ppermute | solution.py:94
  5.6 2.3 %shard_map.105.refs_0_ = bf16[512,512]{1,0:T(8,128)(2,1)} custom-call(bf16[512,2048]{1,0:T(8,128)(2,1)} %train_ref.11, bf16[16,512]{1,0:T(8,128)(2,1)} %bitcast.5, bf16[16,2048]{1,0:T(8,128)(2,1)} %high_ref.11), custom_call_target="tpu_custom_call" | custom-call | flops 8388608 | bytes 1048576 | tf_op jit(solution)/shard_map/pallas_call | solution.py:33
  7.9 0.0 collective-permute-start.3
  8.0 5.0 %collective-permute-done.refs_1_ = bf16[256,512]{1,0:T(8,128)(2,1)S(1)} collective-permute-done((bf16[256,512]{1,0:T(8,128)(2,1)}, bf16[256,512]{1,0:T(8,128)(2,1)S(1)}, u32[]{:S(2)}, u32[]{:S(2)}) %collective-permute-start) | collective-permute-done | bytes 262176 | tf_op jit(solution)/shard_map/ppermute | solution.py:94
  13.0 0.0 collective-permute-start.2
  13.0 0.5 collective-permute-start.4
  13.5 0.0 collective-permute-done.1.refs_2_
  13.5 1.0 collective-permute-done.2.refs_3_
  14.5 0.7 copy-done.20
  15.2 2.0 %shard_map.107.refs_4_ = bf16[2048,2048]{1,0:T(8,128)(2,1)} custom-call(bf16[256,512]{1,0:T(8,128)(2,1)} %shard_map.106.refs_0_, bf16[256,512]{1,0:T(8,128)(2,1)} %copy-done.18, bf16[256,512]{1,0:T(8,128)(2,1)} %copy-done.19, bf16[256,512]{1,0:T(8,128)(2,1)} %copy-done.20), custom_call_target="tpu_custom_call" | custom-call | bytes 2097152 | tf_op jit(solution)/shard_map/pallas_call | solution.py:76
  17.2 6.2 %collective-permute-done.3.refs_1_ = bf16[512,512]{1,0:T(8,128)(2,1)S(1)} collective-permute-done((bf16[512,512]{1,0:T(8,128)(2,1)}, bf16[512,512]{1,0:T(8,128)(2,1)S(1)}, u32[]{:S(2)}, u32[]{:S(2)}) %collective-permute-start.3) | collective-permute-done | bytes 524320 | tf_op jit(solution)/shard_map/ppermute | solution.py:94
  23.4 0.0 collective-permute-start.5
  23.4 2.5 %shard_map.104.refs_0_ = bf16[512,512]{1,0:T(8,128)(2,1)} custom-call(bf16[512,2048]{1,0:T(8,128)(2,1)} %train_ref.11, bf16[16,512]{1,0:T(8,128)(2,1)} %bitcast.6, bf16[16,2048]{1,0:T(8,128)(2,1)} %high_ref.11), custom_call_target="tpu_custom_call" | custom-call | flops 8388608 | bytes 1048576 | tf_op jit(solution)/shard_map/pallas_call | solution.py:33
  25.9 1.7 %collective-permute-start.6 = (bf16[512,512]{1,0:T(8,128)(2,1)}, bf16[512,512]{1,0:T(8,128)(2,1)S(1)}, u32[]{:S(2)}, u32[]{:S(2)}) collective-permute-start(bf16[512,512]{1,0:T(8,128)(2,1)} %shard_map.104.refs_0_), channel_id=1, source_target_pairs={{0,8},{4,12},{8,0},{12,4},{1,9},{5,13},{9,1},{13,5},{2,10},{6,14},... | collective-permute-start | bytes 1572872 | tf_op jit(solution)/shard_map/ppermute | solution.py:94
  27.6 3.4 %shard_map.103.refs_0_ = bf16[768,512]{1,0:T(8,128)(2,1)} custom-call(bf16[512,2048]{1,0:T(8,128)(2,1)} %train_ref.11, bf16[16,512]{1,0:T(8,128)(2,1)} %bitcast.7, bf16[16,2048]{1,0:T(8,128)(2,1)} %high_ref.11), custom_call_target="tpu_custom_call" | custom-call | flops 12582912 | bytes 1572864 | tf_op jit(solution)/shard_map/pallas_call | solution.py:33
  31.0 0.3 collective-permute-start.9
  31.3 0.8 copy-done.12
  32.1 2.4 %shard_map.108.refs_4_ = bf16[2048,2048]{1,0:T(8,128)(2,1)} custom-call(bf16[512,512]{1,0:T(8,128)(2,1)} %shard_map.105.refs_0_, bf16[512,512]{1,0:T(8,128)(2,1)} %copy-done.10, bf16[512,512]{1,0:T(8,128)(2,1)} %copy-done.12, bf16[512,512]{1,0:T(8,128)(2,1)} %collective-permute-done.5.refs_3_, ...), custom_call_target="tpu_custom_call", output_to_operand_aliasing={{}: (4, {})} | custom-call | bytes 4194304 | tf_op jit(solution)/shard_map/pallas_call | solution.py:76
  34.5 6.4 %collective-permute-done.6.refs_1_ = bf16[512,512]{1,0:T(8,128)(2,1)S(1)} collective-permute-done((bf16[512,512]{1,0:T(8,128)(2,1)}, bf16[512,512]{1,0:T(8,128)(2,1)S(1)}, u32[]{:S(2)}, u32[]{:S(2)}) %collective-permute-start.6) | collective-permute-done | bytes 524320 | tf_op jit(solution)/shard_map/ppermute | solution.py:94
  40.9 0.5 collective-permute-start.10
  41.4 1.5 %collective-permute-done.8.refs_3_ = bf16[512,512]{1,0:T(8,128)(2,1)} collective-permute-done((bf16[512,512]{1,0:T(8,128)(2,1)S(1)}, bf16[512,512]{1,0:T(8,128)(2,1)}, u32[]{:S(2)}, u32[]{:S(2)}) %collective-permute-start.8) | collective-permute-done | bytes 524320 | tf_op jit(solution)/shard_map/ppermute | solution.py:94
  42.9 2.4 %shard_map.109.refs_4_ = bf16[2048,2048]{1,0:T(8,128)(2,1)} custom-call(bf16[512,512]{1,0:T(8,128)(2,1)} %shard_map.104.refs_0_, bf16[512,512]{1,0:T(8,128)(2,1)} %copy-done.13, bf16[512,512]{1,0:T(8,128)(2,1)} %collective-permute-done.7.refs_2_, bf16[512,512]{1,0:T(8,128)(2,1)} %collective-permute-done.8.refs_3_, ...), custom_call_target="tpu_custom_call", output_to_operand_aliasing={{}: (4, {})} | custom-call | bytes 4194304 | tf_op jit(solution)/shard_map/pallas_call | solution.py:76
  45.4 11.7 %collective-permute-done.9.refs_1_ = bf16[768,512]{1,0:T(8,128)(2,1)S(1)} collective-permute-done((bf16[768,512]{1,0:T(8,128)(2,1)}, bf16[768,512]{1,0:T(8,128)(2,1)S(1)}, u32[]{:S(2)}, u32[]{:S(2)}) %collective-permute-start.9) | collective-permute-done | bytes 786464 | tf_op jit(solution)/shard_map/ppermute | solution.py:94
  57.1 3.6 %shard_map.111.refs_0_ = bf16[768,512]{1,0:T(8,128)(2,1)} custom-call(bf16[512,2048]{1,0:T(8,128)(2,1)} %train_ref.15, bf16[16,512]{1,0:T(8,128)(2,1)} %bitcast.8, bf16[16,2048]{1,0:T(8,128)(2,1)} %high_ref.15), custom_call_target="tpu_custom_call" | custom-call | flops 12582912 | bytes 1572864 | tf_op jit(solution)/shard_map/pallas_call | solution.py:33
  60.7 1.7 %collective-permute-start.12 = (bf16[768,512]{1,0:T(8,128)(2,1)}, bf16[768,512]{1,0:T(8,128)(2,1)}, u32[]{:S(2)}, u32[]{:S(2)}) collective-permute-start(bf16[768,512]{1,0:T(8,128)(2,1)} %shard_map.111.refs_0_), channel_id=1, source_target_pairs={{0,8},{4,12},{8,0},{12,4},{1,9},{5,13},{9,1},{13,5},{2,10},{6,14},... | collective-permute-start | bytes 2359304 | tf_op jit(solution)/shard_map/ppermute | solution.py:94
  62.4 0.0 collective-permute-start.13
  62.5 0.9 copy-done.3
  63.3 0.9 copy-done.4
  64.2 2.9 %shard_map.110 = bf16[2048,2048]{1,0:T(8,128)(2,1)} custom-call(bf16[768,512]{1,0:T(8,128)(2,1)} %shard_map.103.refs_0_, bf16[768,512]{1,0:T(8,128)(2,1)} %copy-done.2, bf16[768,512]{1,0:T(8,128)(2,1)} %copy-done.3, bf16[768,512]{1,0:T(8,128)(2,1)} %copy-done.4, bf16[2048,2048]{1,0:T(8,128)(2,1)} %shard_map.109.refs_4_), custom_call_target="tpu_custom_call", output_to_operand_aliasing={{}: (4, {})} | custom-call | bytes 6291456 | tf_op jit(solution)/shard_map/pallas_call | solution.py:76
  67.1 13.7 %collective-permute-done.12.refs_1_ = bf16[768,512]{1,0:T(8,128)(2,1)} collective-permute-done((bf16[768,512]{1,0:T(8,128)(2,1)}, bf16[768,512]{1,0:T(8,128)(2,1)}, u32[]{:S(2)}, u32[]{:S(2)}) %collective-permute-start.12) | collective-permute-done | bytes 786464 | tf_op jit(solution)/shard_map/ppermute | solution.py:94
  80.7 2.3 %shard_map.114.refs_0_ = bf16[512,512]{1,0:T(8,128)(2,1)} custom-call(bf16[512,2048]{1,0:T(8,128)(2,1)} %train_ref.15, bf16[16,512]{1,0:T(8,128)(2,1)} %bitcast.9, bf16[16,2048]{1,0:T(8,128)(2,1)} %high_ref.15), custom_call_target="tpu_custom_call" | custom-call | flops 8388608 | bytes 1048576 | tf_op jit(solution)/shard_map/pallas_call | solution.py:33
  83.1 1.7 %collective-permute-start.15 = (bf16[512,512]{1,0:T(8,128)(2,1)}, bf16[512,512]{1,0:T(8,128)(2,1)S(1)}, u32[]{:S(2)}, u32[]{:S(2)}) collective-permute-start(bf16[512,512]{1,0:T(8,128)(2,1)} %shard_map.114.refs_0_), channel_id=1, source_target_pairs={{0,8},{4,12},{8,0},{12,4},{1,9},{5,13},{9,1},{13,5},{2,10},{6,14},... | collective-permute-start | bytes 1572872 | tf_op jit(solution)/shard_map/ppermute | solution.py:94
  84.8 0.2 collective-permute-start.16
  85.0 0.9 copy-done.5
  85.9 2.9 %shard_map.115.refs_4_ = bf16[2048,2048]{1,0:T(8,128)(2,1)} custom-call(bf16[768,512]{1,0:T(8,128)(2,1)} %shard_map.111.refs_0_, bf16[768,512]{1,0:T(8,128)(2,1)} %collective-permute-done.12.refs_1_, bf16[768,512]{1,0:T(8,128)(2,1)} %collective-permute-done.13.refs_2_, bf16[768,512]{1,0:T(8,128)(2,1)} %copy-done.5), custom_call_target="tpu_custom_call" | custom-call | bytes 6291456 | tf_op jit(solution)/shard_map/pallas_call | solution.py:76
  88.8 8.8 %collective-permute-done.15.refs_1_ = bf16[512,512]{1,0:T(8,128)(2,1)S(1)} collective-permute-done((bf16[512,512]{1,0:T(8,128)(2,1)}, bf16[512,512]{1,0:T(8,128)(2,1)S(1)}, u32[]{:S(2)}, u32[]{:S(2)}) %collective-permute-start.15) | collective-permute-done | bytes 524320 | tf_op jit(solution)/shard_map/ppermute | solution.py:94
  97.6 2.5 %shard_map.113.refs_0_ = bf16[512,512]{1,0:T(8,128)(2,1)} custom-call(bf16[512,2048]{1,0:T(8,128)(2,1)} %train_ref.15, bf16[16,512]{1,0:T(8,128)(2,1)} %bitcast.10, bf16[16,2048]{1,0:T(8,128)(2,1)} %high_ref.15), custom_call_target="tpu_custom_call" | custom-call | flops 8388608 | bytes 1048576 | tf_op jit(solution)/shard_map/pallas_call | solution.py:33
  100.1 1.7 %collective-permute-start.18 = (bf16[512,512]{1,0:T(8,128)(2,1)}, bf16[512,512]{1,0:T(8,128)(2,1)S(1)}, u32[]{:S(2)}, u32[]{:S(2)}) collective-permute-start(bf16[512,512]{1,0:T(8,128)(2,1)} %shard_map.113.refs_0_), channel_id=1, source_target_pairs={{0,8},{4,12},{8,0},{12,4},{1,9},{5,13},{9,1},{13,5},{2,10},{6,14},... | collective-permute-start | bytes 1572872 | tf_op jit(solution)/shard_map/ppermute | solution.py:94
  101.9 0.0 collective-permute-start.19
  101.9 2.0 %shard_map.112.refs_0_ = bf16[256,512]{1,0:T(8,128)(2,1)} custom-call(bf16[512,2048]{1,0:T(8,128)(2,1)} %train_ref.15, bf16[16,512]{1,0:T(8,128)(2,1)} %bitcast.11, bf16[16,2048]{1,0:T(8,128)(2,1)} %high_ref.15), custom_call_target="tpu_custom_call" | custom-call | flops 4194304 | bytes 524288 | tf_op jit(solution)/shard_map/pallas_call | solution.py:33
  103.9 0.3 collective-permute-start.21
  104.3 0.8 copy-done.9
  105.0 0.8 copy-done.11
  105.8 2.4 %shard_map.116.refs_4_ = bf16[2048,2048]{1,0:T(8,128)(2,1)} custom-call(bf16[512,512]{1,0:T(8,128)(2,1)} %shard_map.114.refs_0_, bf16[512,512]{1,0:T(8,128)(2,1)} %copy-done.8, bf16[512,512]{1,0:T(8,128)(2,1)} %copy-done.9, bf16[512,512]{1,0:T(8,128)(2,1)} %copy-done.11, bf16[2048,2048]{1,0:T(8,128)(2,1)} %shard_map.115.refs_4_), custom_call_target="tpu_custom_call", output_to_operand_aliasing={{}: (4, {})} | custom-call | bytes 4194304 | tf_op jit(solution)/shard_map/pallas_call | solution.py:76
  108.3 6.9 %collective-permute-done.18.refs_1_ = bf16[512,512]{1,0:T(8,128)(2,1)S(1)} collective-permute-done((bf16[512,512]{1,0:T(8,128)(2,1)}, bf16[512,512]{1,0:T(8,128)(2,1)S(1)}, u32[]{:S(2)}, u32[]{:S(2)}) %collective-permute-start.18) | collective-permute-done | bytes 524320 | tf_op jit(solution)/shard_map/ppermute | solution.py:94
  115.2 0.1 broadcast_select_fusion
  115.2 1.8 %collective-permute-start.24 = (bf16[16,128]{1,0:T(8,128)(2,1)S(1)}, bf16[16,128]{1,0:T(8,128)(2,1)S(1)}, u32[]{:S(2)}, u32[]{:S(2)}) collective-permute-start(bf16[16,128]{1,0:T(8,128)(2,1)S(1)} %broadcast_select_fusion), channel_id=1, source_target_pairs={{0,1},{1,0},{2,3},{3,2},{4,5},{5,4},{6,7},{7,6},{8,9},{9,8},{10,11... | collective-permute-start | bytes 12296 | tf_op jit(solution)/shard_map/ppermute | solution.py:94
  117.0 1.8 %collective-permute-done.24 = bf16[16,128]{1,0:T(8,128)(2,1)S(1)} collective-permute-done((bf16[16,128]{1,0:T(8,128)(2,1)S(1)}, bf16[16,128]{1,0:T(8,128)(2,1)S(1)}, u32[]{:S(2)}, u32[]{:S(2)}) %collective-permute-start.24) | collective-permute-done | bytes 4128 | tf_op jit(solution)/shard_map/ppermute | solution.py:94
  118.8 0.1 fusion
  118.9 2.8 %collective-permute-start.25 = (bf16[16,128]{1,0:T(8,128)(2,1)S(1)}, bf16[16,128]{1,0:T(8,128)(2,1)S(1)}, u32[]{:S(2)}, u32[]{:S(2)}) collective-permute-start(bf16[16,128]{1,0:T(8,128)(2,1)S(1)} %fusion), channel_id=1, source_target_pairs={{0,2},{1,3},{2,0},{3,1},{4,6},{5,7},{6,4},{7,5},{8,10},{9,11},{10,... | collective-permute-start | bytes 12296 | tf_op jit(solution)/shard_map/ppermute | solution.py:94
  121.8 0.8 copy-done.7
  122.6 0.8 copy-done.14
  123.4 2.4 %shard_map.117.refs_4_ = bf16[2048,2048]{1,0:T(8,128)(2,1)} custom-call(bf16[512,512]{1,0:T(8,128)(2,1)} %shard_map.113.refs_0_, bf16[512,512]{1,0:T(8,128)(2,1)} %copy-done.6, bf16[512,512]{1,0:T(8,128)(2,1)} %copy-done.7, bf16[512,512]{1,0:T(8,128)(2,1)} %copy-done.14, bf16[2048,2048]{1,0:T(8,128)(2,1)} %shard_map.116.refs_4_), custom_call_target="tpu_custom_call", output_to_operand_aliasing={{}: (4, {})} | custom-call | bytes 4194304 | tf_op jit(solution)/shard_map/pallas_call | solution.py:76
  125.8 0.6 collective-permute-start.23
  126.4 0.1 fusion.1
  126.5 0.0 collective-permute-start.26
  126.5 1.1 collective-permute-done.26
  127.6 1.5 %collective-permute-start.27 = (bf16[16,128]{1,0:T(8,128)(2,1)S(1)}, bf16[16,128]{1,0:T(8,128)(2,1)S(1)}, u32[]{:S(2)}, u32[]{:S(2)}) collective-permute-start(bf16[16,128]{1,0:T(8,128)(2,1)S(1)} %add.22), channel_id=1, source_target_pairs={{0,8},{4,12},{8,0},{12,4},{1,9},{5,13},{9,1},{13,5},{2,10},{6,14},... | collective-permute-start | bytes 12296 | tf_op jit(solution)/shard_map/ppermute | solution.py:94
  129.2 2.1 %collective-permute-done.27 = bf16[16,128]{1,0:T(8,128)(2,1)S(1)} collective-permute-done((bf16[16,128]{1,0:T(8,128)(2,1)S(1)}, bf16[16,128]{1,0:T(8,128)(2,1)S(1)}, u32[]{:S(2)}, u32[]{:S(2)}) %collective-permute-start.27) | collective-permute-done | bytes 4128 | tf_op jit(solution)/shard_map/ppermute | solution.py:94
  131.2 0.6 add_bitcast_fusion
  131.9 0.7 copy-done.16
  132.6 0.7 copy-done.17
  133.3 2.0 %shard_map.118 = bf16[2048,2048]{1,0:T(8,128)(2,1)} custom-call(bf16[256,512]{1,0:T(8,128)(2,1)} %shard_map.112.refs_0_, bf16[256,512]{1,0:T(8,128)(2,1)} %copy-done.15, bf16[256,512]{1,0:T(8,128)(2,1)} %copy-done.16, bf16[256,512]{1,0:T(8,128)(2,1)} %copy-done.17, bf16[2048,2048]{1,0:T(8,128)(2,1)} %shard_map.117.refs_4_), custom_call_target="tpu_custom_call", output_to_operand_aliasing={{}: (4, {})} | custom-call | bytes 2097152 | tf_op jit(solution)/shard_map/pallas_call | solution.py:76
  (61 shorter events, 0.1 us)
Async XLA Ops:
  2.6 10.4 %collective-permute-start = (bf16[256,512]{1,0:T(8,128)(2,1)}, bf16[256,512]{1,0:T(8,128)(2,1)S(1)}, u32[]{:S(2)}, u32[]{:S(2)}) collective-permute-start(bf16[256,512]{1,0:T(8,128)(2,1)} %shard_map.106.refs_0_), channel_id=1, source_target_pairs={{0,8},{4,12},{8,0},{12,4},{1,9},{5,13},{9,1},{13,5},{2,10},{6,14},... | collective-permute-start | bytes 786440 | tf_op jit(solution)/shard_map/ppermute | solution.py:94
  7.9 15.4 %collective-permute-start.3 = (bf16[512,512]{1,0:T(8,128)(2,1)}, bf16[512,512]{1,0:T(8,128)(2,1)S(1)}, u32[]{:S(2)}, u32[]{:S(2)}) collective-permute-start(bf16[512,512]{1,0:T(8,128)(2,1)} %shard_map.105.refs_0_), channel_id=1, source_target_pairs={{0,8},{4,12},{8,0},{12,4},{1,9},{5,13},{9,1},{13,5},{2,10},{6,14},... | collective-permute-start | bytes 1572872 | tf_op jit(solution)/shard_map/ppermute | solution.py:94
  8.0 5.5 %collective-permute-start.1 = (bf16[256,512]{1,0:T(8,128)(2,1)}, bf16[256,512]{1,0:T(8,128)(2,1)S(1)}, u32[]{:S(2)}, u32[]{:S(2)}) collective-permute-start(bf16[256,512]{1,0:T(8,128)(2,1)} %shard_map.106.refs_0_), channel_id=1, source_target_pairs={{0,4},{4,0},{8,12},{12,8},{1,5},{5,1},{9,13},{13,9},{2,6},{6,2},{1... | collective-permute-start | bytes 786440 | tf_op jit(solution)/shard_map/ppermute | solution.py:94
  13.0 1.5 %copy-start.18 = (bf16[256,512]{1,0:T(8,128)(2,1)}, bf16[256,512]{1,0:T(8,128)(2,1)S(1)}, u32[]{:S(2)}) copy-start(bf16[256,512]{1,0:T(8,128)(2,1)S(1)} %collective-permute-done.refs_1_) | copy-start | bytes 786436
  13.0 1.5 %collective-permute-start.2 = (bf16[256,512]{1,0:T(8,128)(2,1)S(1)}, bf16[256,512]{1,0:T(8,128)(2,1)S(1)}, u32[]{:S(2)}, u32[]{:S(2)}) collective-permute-start(bf16[256,512]{1,0:T(8,128)(2,1)S(1)} %collective-permute-done.refs_1_), channel_id=1, source_target_pairs={{0,4},{4,0},{8,12},{12,8},{1,5},{5,1},{9,13},{13,9},{2,6},{6,2},{1... | collective-permute-start | bytes 786440 | tf_op jit(solution)/shard_map/ppermute | solution.py:94
  13.0 18.3 %collective-permute-start.4 = (bf16[512,512]{1,0:T(8,128)(2,1)}, bf16[512,512]{1,0:T(8,128)(2,1)S(1)}, u32[]{:S(2)}, u32[]{:S(2)}) collective-permute-start(bf16[512,512]{1,0:T(8,128)(2,1)} %shard_map.105.refs_0_), channel_id=1, source_target_pairs={{0,4},{4,0},{8,12},{12,8},{1,5},{5,1},{9,13},{13,9},{2,6},{6,2},{1... | collective-permute-start | bytes 1572872 | tf_op jit(solution)/shard_map/ppermute | solution.py:94
  13.5 1.0 copy-start.19
  14.5 0.7 copy-start.20
  23.4 7.9 %copy-start.10 = (bf16[512,512]{1,0:T(8,128)(2,1)}, bf16[512,512]{1,0:T(8,128)(2,1)S(1)}, u32[]{:S(2)}) copy-start(bf16[512,512]{1,0:T(8,128)(2,1)S(1)} %collective-permute-done.3.refs_1_) | copy-start | bytes 1572868
  23.4 7.9 %collective-permute-start.5 = (bf16[512,512]{1,0:T(8,128)(2,1)S(1)}, bf16[512,512]{1,0:T(8,128)(2,1)}, u32[]{:S(2)}, u32[]{:S(2)}) collective-permute-start(bf16[512,512]{1,0:T(8,128)(2,1)S(1)} %collective-permute-done.3.refs_1_), channel_id=1, source_target_pairs={{0,4},{4,0},{8,12},{12,8},{1,5},{5,1},{9,13},{13,9},{2,6},{6,2},{1... | collective-permute-start | bytes 1572872 | tf_op jit(solution)/shard_map/ppermute | solution.py:94
  25.9 15.0 %collective-permute-start.6 = (bf16[512,512]{1,0:T(8,128)(2,1)}, bf16[512,512]{1,0:T(8,128)(2,1)S(1)}, u32[]{:S(2)}, u32[]{:S(2)}) collective-permute-start(bf16[512,512]{1,0:T(8,128)(2,1)} %shard_map.104.refs_0_), channel_id=1, source_target_pairs={{0,8},{4,12},{8,0},{12,4},{1,9},{5,13},{9,1},{13,5},{2,10},{6,14},... | collective-permute-start | bytes 1572872 | tf_op jit(solution)/shard_map/ppermute | solution.py:94
  31.0 9.9 %copy-start = (bf16[768,512]{1,0:T(8,128)(2,1)S(1)}, bf16[768,512]{1,0:T(8,128)(2,1)}, u32[]{:S(2)}) copy-start(bf16[768,512]{1,0:T(8,128)(2,1)} %shard_map.103.refs_0_) | copy-start | bytes 2359300
  31.0 26.1 %collective-permute-start.9 = (bf16[768,512]{1,0:T(8,128)(2,1)}, bf16[768,512]{1,0:T(8,128)(2,1)S(1)}, u32[]{:S(2)}, u32[]{:S(2)}) collective-permute-start(bf16[768,512]{1,0:T(8,128)(2,1)} %shard_map.103.refs_0_), channel_id=1, source_target_pairs={{0,8},{4,12},{8,0},{12,4},{1,9},{5,13},{9,1},{13,5},{2,10},{6,14},... | collective-permute-start | bytes 2359304 | tf_op jit(solution)/shard_map/ppermute | solution.py:94
  31.3 10.1 %collective-permute-start.7 = (bf16[512,512]{1,0:T(8,128)(2,1)}, bf16[512,512]{1,0:T(8,128)(2,1)}, u32[]{:S(2)}, u32[]{:S(2)}) collective-permute-start(bf16[512,512]{1,0:T(8,128)(2,1)} %shard_map.104.refs_0_), channel_id=1, source_target_pairs={{0,4},{4,0},{8,12},{12,8},{1,5},{5,1},{9,13},{13,9},{2,6},{6,2},{1... | collective-permute-start | bytes 1572872 | tf_op jit(solution)/shard_map/ppermute | solution.py:94
  31.3 0.8 copy-start.12
  40.9 2.0 %copy-start.13 = (bf16[512,512]{1,0:T(8,128)(2,1)}, bf16[512,512]{1,0:T(8,128)(2,1)S(1)}, u32[]{:S(2)}) copy-start(bf16[512,512]{1,0:T(8,128)(2,1)S(1)} %collective-permute-done.6.refs_1_) | copy-start | bytes 1572868
  40.9 2.0 %collective-permute-start.8 = (bf16[512,512]{1,0:T(8,128)(2,1)S(1)}, bf16[512,512]{1,0:T(8,128)(2,1)}, u32[]{:S(2)}, u32[]{:S(2)}) collective-permute-start(bf16[512,512]{1,0:T(8,128)(2,1)S(1)} %collective-permute-done.6.refs_1_), channel_id=1, source_target_pairs={{0,4},{4,0},{8,12},{12,8},{1,5},{5,1},{9,13},{13,9},{2,6},{6,2},{1... | collective-permute-start | bytes 1572872 | tf_op jit(solution)/shard_map/ppermute | solution.py:94
  40.9 21.5 %collective-permute-start.10 = (bf16[768,512]{1,0:T(8,128)(2,1)S(1)}, bf16[768,512]{1,0:T(8,128)(2,1)S(1)}, u32[]{:S(2)}, u32[]{:S(2)}) collective-permute-start(bf16[768,512]{1,0:T(8,128)(2,1)S(1)} %copy-done), channel_id=1, source_target_pairs={{0,4},{4,0},{8,12},{12,8},{1,5},{5,1},{9,13},{13,9},{2,6},{6,2},{1... | collective-permute-start | bytes 2359304 | tf_op jit(solution)/shard_map/ppermute | solution.py:94
  57.1 5.4 %copy-start.2 = (bf16[768,512]{1,0:T(8,128)(2,1)}, bf16[768,512]{1,0:T(8,128)(2,1)S(1)}, u32[]{:S(2)}) copy-start(bf16[768,512]{1,0:T(8,128)(2,1)S(1)} %collective-permute-done.9.refs_1_) | copy-start | bytes 2359300
  57.1 5.3 %collective-permute-start.11 = (bf16[768,512]{1,0:T(8,128)(2,1)S(1)}, bf16[768,512]{1,0:T(8,128)(2,1)S(1)}, u32[]{:S(2)}, u32[]{:S(2)}) collective-permute-start(bf16[768,512]{1,0:T(8,128)(2,1)S(1)} %collective-permute-done.9.refs_1_), channel_id=1, source_target_pairs={{0,4},{4,0},{8,12},{12,8},{1,5},{5,1},{9,13},{13,9},{2,6},{6,2},{1... | collective-permute-start | bytes 2359304 | tf_op jit(solution)/shard_map/ppermute | solution.py:94
  60.7 20.0 %collective-permute-start.12 = (bf16[768,512]{1,0:T(8,128)(2,1)}, bf16[768,512]{1,0:T(8,128)(2,1)}, u32[]{:S(2)}, u32[]{:S(2)}) collective-permute-start(bf16[768,512]{1,0:T(8,128)(2,1)} %shard_map.111.refs_0_), channel_id=1, source_target_pairs={{0,8},{4,12},{8,0},{12,4},{1,9},{5,13},{9,1},{13,5},{2,10},{6,14},... | collective-permute-start | bytes 2359304 | tf_op jit(solution)/shard_map/ppermute | solution.py:94
  62.4 22.6 %collective-permute-start.13 = (bf16[768,512]{1,0:T(8,128)(2,1)}, bf16[768,512]{1,0:T(8,128)(2,1)}, u32[]{:S(2)}, u32[]{:S(2)}) collective-permute-start(bf16[768,512]{1,0:T(8,128)(2,1)} %shard_map.111.refs_0_), channel_id=1, source_target_pairs={{0,4},{4,0},{8,12},{12,8},{1,5},{5,1},{9,13},{13,9},{2,6},{6,2},{1... | collective-permute-start | bytes 2359304 | tf_op jit(solution)/shard_map/ppermute | solution.py:94
  62.4 0.9 copy-start.3
  63.3 0.9 copy-start.4
  80.7 4.3 %collective-permute-start.14 = (bf16[768,512]{1,0:T(8,128)(2,1)}, bf16[768,512]{1,0:T(8,128)(2,1)S(1)}, u32[]{:S(2)}, u32[]{:S(2)}) collective-permute-start(bf16[768,512]{1,0:T(8,128)(2,1)} %collective-permute-done.12.refs_1_), channel_id=1, source_target_pairs={{0,4},{4,0},{8,12},{12,8},{1,5},{5,1},{9,13},{13,9},{2,6},{6,2},{1... | collective-permute-start | bytes 2359304 | tf_op jit(solution)/shard_map/ppermute | solution.py:94
  83.0 21.1 %copy-start.21 = (f32[128]{0:T(128)S(1)}, f32[128]{0:T(128)}, u32[]{:S(2)}) copy-start(f32[128]{0:T(128)} %param.14) | copy-start | bytes 1540
  83.0 21.1 %copy-start.22 = (f32[128]{0:T(128)S(1)}, f32[128]{0:T(128)}, u32[]{:S(2)}) copy-start(f32[128]{0:T(128)} %param.15) | copy-start | bytes 1540
  83.1 14.5 %collective-permute-start.15 = (bf16[512,512]{1,0:T(8,128)(2,1)}, bf16[512,512]{1,0:T(8,128)(2,1)S(1)}, u32[]{:S(2)}, u32[]{:S(2)}) collective-permute-start(bf16[512,512]{1,0:T(8,128)(2,1)} %shard_map.114.refs_0_), channel_id=1, source_target_pairs={{0,8},{4,12},{8,0},{12,4},{1,9},{5,13},{9,1},{13,5},{2,10},{6,14},... | collective-permute-start | bytes 1572872 | tf_op jit(solution)/shard_map/ppermute | solution.py:94
  84.8 19.4 %collective-permute-start.16 = (bf16[512,512]{1,0:T(8,128)(2,1)}, bf16[512,512]{1,0:T(8,128)(2,1)S(1)}, u32[]{:S(2)}, u32[]{:S(2)}) collective-permute-start(bf16[512,512]{1,0:T(8,128)(2,1)} %shard_map.114.refs_0_), channel_id=1, source_target_pairs={{0,4},{4,0},{8,12},{12,8},{1,5},{5,1},{9,13},{13,9},{2,6},{6,2},{1... | collective-permute-start | bytes 1572872 | tf_op jit(solution)/shard_map/ppermute | solution.py:94
  85.0 0.9 copy-start.5
  97.6 6.7 %copy-start.8 = (bf16[512,512]{1,0:T(8,128)(2,1)}, bf16[512,512]{1,0:T(8,128)(2,1)S(1)}, u32[]{:S(2)}) copy-start(bf16[512,512]{1,0:T(8,128)(2,1)S(1)} %collective-permute-done.15.refs_1_) | copy-start | bytes 1572868
  97.6 6.6 %collective-permute-start.17 = (bf16[512,512]{1,0:T(8,128)(2,1)S(1)}, bf16[512,512]{1,0:T(8,128)(2,1)S(1)}, u32[]{:S(2)}, u32[]{:S(2)}) collective-permute-start(bf16[512,512]{1,0:T(8,128)(2,1)S(1)} %collective-permute-done.15.refs_1_), channel_id=1, source_target_pairs={{0,4},{4,0},{8,12},{12,8},{1,5},{5,1},{9,13},{13,9},{2,6},{6,2},{1... | collective-permute-start | bytes 1572872 | tf_op jit(solution)/shard_map/ppermute | solution.py:94
  100.1 15.0 %collective-permute-start.18 = (bf16[512,512]{1,0:T(8,128)(2,1)}, bf16[512,512]{1,0:T(8,128)(2,1)S(1)}, u32[]{:S(2)}, u32[]{:S(2)}) collective-permute-start(bf16[512,512]{1,0:T(8,128)(2,1)} %shard_map.113.refs_0_), channel_id=1, source_target_pairs={{0,8},{4,12},{8,0},{12,4},{1,9},{5,13},{9,1},{13,5},{2,10},{6,14},... | collective-permute-start | bytes 1572872 | tf_op jit(solution)/shard_map/ppermute | solution.py:94
  101.9 19.9 %collective-permute-start.19 = (bf16[512,512]{1,0:T(8,128)(2,1)}, bf16[512,512]{1,0:T(8,128)(2,1)S(1)}, u32[]{:S(2)}, u32[]{:S(2)}) collective-permute-start(bf16[512,512]{1,0:T(8,128)(2,1)} %shard_map.113.refs_0_), channel_id=1, source_target_pairs={{0,4},{4,0},{8,12},{12,8},{1,5},{5,1},{9,13},{13,9},{2,6},{6,2},{1... | collective-permute-start | bytes 1572872 | tf_op jit(solution)/shard_map/ppermute | solution.py:94
  103.9 21.9 %collective-permute-start.21 = (bf16[256,512]{1,0:T(8,128)(2,1)}, bf16[256,512]{1,0:T(8,128)(2,1)S(1)}, u32[]{:S(2)}, u32[]{:S(2)}) collective-permute-start(bf16[256,512]{1,0:T(8,128)(2,1)} %shard_map.112.refs_0_), channel_id=1, source_target_pairs={{0,8},{4,12},{8,0},{12,4},{1,9},{5,13},{9,1},{13,5},{2,10},{6,14},... | collective-permute-start | bytes 786440 | tf_op jit(solution)/shard_map/ppermute | solution.py:94
  104.2 17.5 %copy-start.1 = (bf16[256,512]{1,0:T(8,128)(2,1)S(1)}, bf16[256,512]{1,0:T(8,128)(2,1)}, u32[]{:S(2)}) copy-start(bf16[256,512]{1,0:T(8,128)(2,1)} %shard_map.112.refs_0_) | copy-start | bytes 786436
  104.2 0.8 copy-start.9
  105.0 0.8 copy-start.11
  115.1 6.6 %copy-start.6 = (bf16[512,512]{1,0:T(8,128)(2,1)}, bf16[512,512]{1,0:T(8,128)(2,1)S(1)}, u32[]{:S(2)}) copy-start(bf16[512,512]{1,0:T(8,128)(2,1)S(1)} %collective-permute-done.18.refs_1_) | copy-start | bytes 1572868
  115.1 6.6 %collective-permute-start.20 = (bf16[512,512]{1,0:T(8,128)(2,1)S(1)}, bf16[512,512]{1,0:T(8,128)(2,1)S(1)}, u32[]{:S(2)}, u32[]{:S(2)}) collective-permute-start(bf16[512,512]{1,0:T(8,128)(2,1)S(1)} %collective-permute-done.18.refs_1_), channel_id=1, source_target_pairs={{0,4},{4,0},{8,12},{12,8},{1,5},{5,1},{9,13},{13,9},{2,6},{6,2},{1... | collective-permute-start | bytes 1572872 | tf_op jit(solution)/shard_map/ppermute | solution.py:94
  115.2 3.6 %collective-permute-start.24 = (bf16[16,128]{1,0:T(8,128)(2,1)S(1)}, bf16[16,128]{1,0:T(8,128)(2,1)S(1)}, u32[]{:S(2)}, u32[]{:S(2)}) collective-permute-start(bf16[16,128]{1,0:T(8,128)(2,1)S(1)} %broadcast_select_fusion), channel_id=1, source_target_pairs={{0,1},{1,0},{2,3},{3,2},{4,5},{5,4},{6,7},{7,6},{8,9},{9,8},{10,11... | collective-permute-start | bytes 12296 | tf_op jit(solution)/shard_map/ppermute | solution.py:94
  118.9 7.5 %collective-permute-start.25 = (bf16[16,128]{1,0:T(8,128)(2,1)S(1)}, bf16[16,128]{1,0:T(8,128)(2,1)S(1)}, u32[]{:S(2)}, u32[]{:S(2)}) collective-permute-start(bf16[16,128]{1,0:T(8,128)(2,1)S(1)} %fusion), channel_id=1, source_target_pairs={{0,2},{1,3},{2,0},{3,1},{4,6},{5,7},{6,4},{7,5},{8,10},{9,11},{10,... | collective-permute-start | bytes 12296 | tf_op jit(solution)/shard_map/ppermute | solution.py:94
  121.7 10.1 %collective-permute-start.22 = (bf16[256,512]{1,0:T(8,128)(2,1)S(1)}, bf16[256,512]{1,0:T(8,128)(2,1)S(1)}, u32[]{:S(2)}, u32[]{:S(2)}) collective-permute-start(bf16[256,512]{1,0:T(8,128)(2,1)S(1)} %copy-done.1), channel_id=1, source_target_pairs={{0,4},{4,0},{8,12},{12,8},{1,5},{5,1},{9,13},{13,9},{2,6},{6,2},{1... | collective-permute-start | bytes 786440 | tf_op jit(solution)/shard_map/ppermute | solution.py:94
  121.7 0.8 copy-start.7
  122.6 0.8 copy-start.14
  125.8 6.1 %copy-start.15 = (bf16[256,512]{1,0:T(8,128)(2,1)}, bf16[256,512]{1,0:T(8,128)(2,1)S(1)}, u32[]{:S(2)}) copy-start(bf16[256,512]{1,0:T(8,128)(2,1)S(1)} %collective-permute-done.21.refs_1_) | copy-start | bytes 786436
  125.8 6.0 %collective-permute-start.23 = (bf16[256,512]{1,0:T(8,128)(2,1)S(1)}, bf16[256,512]{1,0:T(8,128)(2,1)S(1)}, u32[]{:S(2)}, u32[]{:S(2)}) collective-permute-start(bf16[256,512]{1,0:T(8,128)(2,1)S(1)} %collective-permute-done.21.refs_1_), channel_id=1, source_target_pairs={{0,4},{4,0},{8,12},{12,8},{1,5},{5,1},{9,13},{13,9},{2,6},{6,2},{1... | collective-permute-start | bytes 786440 | tf_op jit(solution)/shard_map/ppermute | solution.py:94
  126.5 1.2 collective-permute-start.26
  127.6 3.6 %collective-permute-start.27 = (bf16[16,128]{1,0:T(8,128)(2,1)S(1)}, bf16[16,128]{1,0:T(8,128)(2,1)S(1)}, u32[]{:S(2)}, u32[]{:S(2)}) collective-permute-start(bf16[16,128]{1,0:T(8,128)(2,1)S(1)} %add.22), channel_id=1, source_target_pairs={{0,8},{4,12},{8,0},{12,4},{1,9},{5,13},{9,1},{13,5},{2,10},{6,14},... | collective-permute-start | bytes 12296 | tf_op jit(solution)/shard_map/ppermute | solution.py:94
  131.8 0.7 copy-start.16
  132.6 0.7 copy-start.17

commit v2 on v1

v2 whole, which is shorter than its diff:
```python
import functools

import jax
import jax.numpy as jnp
from jax import lax
from jax.experimental import pallas as pl
from jax.experimental.pallas import tpu as pltpu
from jax.sharding import PartitionSpec as P


mix_rate = 2.0
ANY = pl.BlockSpec(memory_space=pl.ANY)
RAW_PARTS = 2
PIECES = (6, 4, 2, 2, 1, 1)
UNITS = sum(PIECES)
GRANT = pltpu.CompilerParams(vmem_limit_bytes=12 * 2**20)


def merge_kernel(train_ref, low_ref, high_ref, out_ref):
    change = lax.dot_general(
        low_ref[...],
        high_ref[...],
        (((0,), (0,)), ((), ())),
        preferred_element_type=jnp.float32,
    )
    fresh = train_ref[...].astype(jnp.float32) + mix_rate * change
    out_ref[...] = fresh.astype(jnp.bfloat16).T


def merge(train, low, high, first, size):
    rank, rows = low.shape
    tile = 256 if first % 256 == 0 and size % 256 == 0 else 128
    skip = first // tile
    return pl.pallas_call(
        merge_kernel,
        grid=(size // tile,),
        in_specs=[
            pl.BlockSpec((rows, tile), lambda i: (0, i + skip)),
            pl.BlockSpec((rank, rows), lambda i: (0, 0)),
            pl.BlockSpec((rank, tile), lambda i: (0, i + skip)),
        ],
        out_specs=pl.BlockSpec((tile, rows), lambda i: (i, 0)),
        out_shape=jax.ShapeDtypeStruct((size, rows), jnp.bfloat16),
        compiler_params=GRANT,
        cost_estimate=pl.CostEstimate(
            flops=2 * size * rows * rank, bytes_accessed=4 * size * rows, transcendentals=0
        ),
    )(train, low, high)


def place_kernel(spots, started, *refs):
    count = len(spots)
    blocks = refs[:count]
    out_ref = refs[count + started]
    held = refs[count + started + 1 : -2]
    in_sem, out_sem = refs[-2:]
    me = lax.axis_index("shard")
    loads, stores = [], []
    for j, block in enumerate(blocks):
        load = pltpu.make_async_copy(block, held[j], in_sem.at[j])
        load.start()
        loads.append(load)
    for j, (mask, first) in enumerate(spots):
        loads[j].wait()
        size, width = blocks[j].shape
        column = pl.multiple_of((me ^ mask) * width, width)
        store = pltpu.make_async_copy(
            held[j], out_ref.at[pl.ds(first, size), pl.ds(column, width)], out_sem.at[j]
        )
        store.start()
        stores.append(store)
    for store in stores:
        store.wait()


def place(whole, shape, blocks, spots):
    started = whole is not None
    count = len(blocks)
    return pl.pallas_call(
        functools.partial(place_kernel, spots, started),
        in_specs=[ANY] * (count + started),
        out_specs=ANY,
        out_shape=jax.ShapeDtypeStruct(shape, jnp.bfloat16),
        scratch_shapes=[
            *[pltpu.VMEM(block.shape, jnp.bfloat16) for block in blocks],
            pltpu.SemaphoreType.DMA((count,)),
            pltpu.SemaphoreType.DMA((count,)),
        ],
        input_output_aliases={count: 0} if started else {},
        compiler_params=GRANT,
        cost_estimate=pl.CostEstimate(
            flops=0, bytes_accessed=4 * sum(b.size for b in blocks), transcendentals=0
        ),
    )(*blocks, *([whole] if started else []))


def swap(x, axis, size, bit):
    return lax.ppermute(x, axis, [(i, i ^ bit) for i in range(size)])


def near(n, held, masks):
    held, masks = [held], [masks]
    bit = n // 4
    while bit:
        held = held + [swap(h, "shard", n, bit) for h in held]
        masks = masks + [m ^ bit for m in masks]
        bit //= 2
    return held, masks


def gathered(n, gate, up):
    train_gate, low_gate, high_gate = gate
    train_up, low_up, high_up = up
    rows, inner = train_gate.shape
    shape = (inner, n * rows)
    far = n // 2
    raw = swap(train_gate, "shard", n, far)
    raw_low = swap(low_gate.T, "shard", n, far)

    pieces, first = [], 0
    for unit in PIECES:
        size = unit * inner // UNITS
        own = merge(train_up, low_up.T, high_up, first, size)
        pieces.append((first, size, own, swap(own, "shard", n, far)))
        first += size
    held, masks = near(n, merge(train_gate, low_gate.T, high_gate, 0, inner), 0)
    whole_gate = place(None, shape, held, tuple((m, 0) for m in masks))
    blocks, spots = [], []
    for first, size, own, _ in pieces:
        held, masks = near(n, own, 0)
        blocks += held
        spots += [(m, first) for m in masks]
    whole_up = place(None, shape, blocks, tuple(spots))

    raw, whole_gate, whole_up = lax.optimization_barrier((raw, whole_gate, whole_up))
    size = inner // RAW_PARTS
    for first in range(0, inner, size):
        part = merge(raw, raw_low, high_gate, first, size)
        held, masks = near(n, part, far)
        whole_gate = place(whole_gate, shape, held, tuple((m, first) for m in masks))
    for k, (first, size, _, part) in enumerate(pieces):
        if k:
            part, whole_up = lax.optimization_barrier((part, whole_up))
        else:
            part, whole_up, whole_gate = lax.optimization_barrier((part, whole_up, whole_gate))
        held, masks = near(n, part, far)
        whole_up = place(whole_up, shape, held, tuple((m, first) for m in masks))
    return whole_gate, whole_up


def norm_gathered(n, m, gain):
    me = lax.axis_index("shard") * m + lax.axis_index("cols")
    held = jnp.where(jnp.arange(n * m)[:, None] == me, gain[None, :], jnp.zeros((), gain.dtype))
    for axis, size in (("cols", m), ("shard", n)):
        bit = 1
        while bit < size:
            held = held + swap(held, axis, size, bit)
            bit *= 2
    return held.reshape(-1)


def plain(train, low, high):
    fresh = train.astype(jnp.float32) + mix_rate * jnp.dot(
        low, high, preferred_element_type=jnp.float32
    )
    return lax.all_gather(fresh.astype(jnp.bfloat16), "shard", axis=0, tiled=True).T


def power(n):
    return n & (n - 1) == 0


def fits(n, m, rows, inner):
    return n > 1 and power(n) and power(m) and rows % 128 == 0 and inner % (128 * UNITS) == 0


def local(n, m, train_gate, low_gate, high_gate, train_up, low_up, high_up, norm_train, norm_step):
    pairs = [(train_gate, low_gate, high_gate), (train_up, low_up, high_up)]
    gain = (norm_train + norm_step).astype(jnp.bfloat16)
    if not fits(n, m, *train_gate.shape):
        serve_gate, serve_up = [plain(*pair) for pair in pairs]
        serve_norm = lax.all_gather(gain, ("shard", "cols"), axis=0, tiled=True)
        return serve_gate, serve_up, serve_norm
    serve_norm = norm_gathered(n, m, gain)
    serve_gate, serve_up = gathered(n, *pairs)
    return serve_gate, serve_up, serve_norm


def solution(mesh):
    n, m = mesh.shape["shard"], mesh.shape["cols"]
    return jax.shard_map(
        functools.partial(local, n, m),
        mesh=mesh,
        in_specs=(
            P(("trial", "shard"), "cols"),
            P(("trial", "shard"), None),
            P("trial", "cols"),
            P(("trial", "shard"), "cols"),
            P(("trial", "shard"), None),
            P("trial", "cols"),
            P(("trial", "shard", "cols")),
            P(("trial", "shard", "cols")),
        ),
        out_specs=(P(("trial", "cols"), None), P(("trial", "cols"), None), P("trial")),
        check_vma=False,
    )
```

time: 136 us -> 126 us (0.926)
  Pallas kernels: 40 us -> 26.2 us
  waiting for transfers between devices: 66.2 us -> 72.3 us
  local copies, waits for them, and re-layouts: 8.71 us -> 4.72 us
  starting transfers between devices: 18.6 us -> 20.3 us
    pallas_call x8 -> x9, Pallas kernels: 20.6 us -> 11.5 us  [merge(): pl.pallas_call(merge_kernel, grid=(size // tile,), in_specs=[pl.BlockSpec...]
    ppermute x28 -> x27, waiting for transfers between devices: 66.2 us -> 72.3 us  [swap(): return lax.ppermute(x, axis, [(i, i ^ bit) for i in range(size)])]
    pallas_call x8 -> x10, Pallas kernels: 19.3 us -> 14.6 us  [place(): pl.pallas_call(functools.partial(place_kernel, spots, started), in_specs=...]
    unnamed x46 -> x18, local copies, waits for them, and re-layouts: 8.71 us -> 4.72 us
    ppermute x28 -> x27, starting transfers between devices: 18.6 us -> 20.3 us  [swap(): return lax.ppermute(x, axis, [(i, i ^ bit) for i in range(size)])]
  transfers between devices with their start and end apart: 28 -> 27, of which waited for: 12 -> 13; matrix products, arithmetic and copies ran while one was open for 1% -> 1% of each run, Pallas kernels for 27% -> 14%
where the time goes in v2:
time: 126 us; the launch traced here: 125 us
  waiting for transfers between devices  72.3 us (57%)
  Pallas kernels  26.2 us (21%)
  starting transfers between devices  20.3 us (16%)
  local copies, waits for them, and re-layouts  4.72 us (4%)
    ppermute x27, waiting for transfers between devices, swap(): return lax.ppermute(x, axis, [(i, i ^ bit) for i in range(size)])  72.3 us
    ppermute x27, starting transfers between devices, swap(): return lax.ppermute(x, axis, [(i, i ^ bit) for i in range(size)])  20.3 us
    pallas_call x10, Pallas kernels, place(): pl.pallas_call(functools.partial(place_kernel, spots, started), in_specs=...  14.6 us
    pallas_call x9, Pallas kernels, merge(): pl.pallas_call(merge_kernel, grid=(size // tile,), in_specs=[pl.BlockSpec...  11.5 us
    unnamed x18, local copies, waits for them, and re-layouts  4.72 us
  transfers between devices with their start and end apart: 27, of which 13 were waited for; matrix products, arithmetic and copies ran while one was open for 1% of the time, Pallas kernels for 14%

profile of v2, /device:TPU:0, one launch (start us, length us, event | category | flops | bytes accessed | tf_op | source)
XLA Modules:
  0.0 125.2 jit_solution(17508714202606487332)
XLA Ops:
  0.6 0.8 copy-done.3
  1.5 0.7 copy-done.5
  2.2 5.5 %shard_map.104.refs_0_ = bf16[2048,512]{1,0:T(8,128)(2,1)S(1)} custom-call(bf16[512,2048]{1,0:T(8,128)(2,1)} %train_ref.8, bf16[16,512]{1,0:T(8,128)(2,1)S(1)} %bitcast.10, bf16[16,2048]{1,0:T(8,128)(2,1)S(1)} %copy-done.3), custom_call_target="tpu_custom_call" | custom-call | flops 33554432 | bytes 4194304 | tf_op jit(solution)/shard_map/pallas_call | solution.py:34
  7.7 0.6 collective-permute-start.2
  8.3 2.6 %collective-permute-start.1 = (bf16[512,2048]{1,0:T(8,128)(2,1)}, bf16[512,2048]{1,0:T(8,128)(2,1)S(1)}, u32[]{:S(2)}, u32[]{:S(2)}) collective-permute-start(bf16[512,2048]{1,0:T(8,128)(2,1)} %train_ref.8), channel_id=1, source_target_pairs={{0,8},{4,12},{8,0},{12,4},{1,9},{5,13},{9,1},{13,5},{2,10},{6,14},... | collective-permute-start | bytes 6291464 | tf_op jit(solution)/shard_map/ppermute | solution.py:98
  10.9 1.6 %copy-done = bf16[512,2048]{1,0:T(8,128)(2,1)S(1)} copy-done((bf16[512,2048]{1,0:T(8,128)(2,1)S(1)}, bf16[512,2048]{1,0:T(8,128)(2,1)}, u32[]{:S(2)}) %copy-start) | copy-done | bytes 2097176
  12.5 0.8 copy-done.1
  13.3 0.7 copy-done.2
  14.0 1.1 shard_map.103.refs_0_
  15.1 0.2 collective-permute-start.3
  15.3 0.3 shard_map.109.refs_8_
  15.6 0.4 collective-permute-start.7
  16.1 0.3 shard_map.110.refs_10_
  16.3 0.2 collective-permute-start.8
  16.6 0.3 shard_map.107.refs_4_
  16.9 0.8 collective-permute-done.7.refs_9_
  17.7 0.2 collective-permute-start.5
  17.8 0.8 shard_map.106.refs_2_
  18.6 0.4 collective-permute-start.4
  19.0 0.3 shard_map.108.refs_6_
  19.3 0.2 collective-permute-start.6
  19.6 1.4 %collective-permute-done.6.refs_7_ = bf16[256,512]{1,0:T(8,128)(2,1)S(1)} collective-permute-done((bf16[256,512]{1,0:T(8,128)(2,1)S(1)}, bf16[256,512]{1,0:T(8,128)(2,1)S(1)}, u32[]{:S(2)}, u32[]{:S(2)}) %collective-permute-start.6) | collective-permute-done | bytes 262176 | tf_op jit(solution)/shard_map/ppermute | solution.py:98
  21.0 0.3 collective-permute-start.9
  21.2 3.1 %shard_map.111.refs_2_ = bf16[2048,2048]{1,0:T(8,128)(2,1)} custom-call(bf16[768,512]{1,0:T(8,128)(2,1)S(1)} %shard_map.103.refs_0_, bf16[768,512]{1,0:T(8,128)(2,1)S(1)} %collective-permute-done.3.refs_1_, bf16[512,512]{1,0:T(8,128)(2,1)S(1)} %shard_map.106.refs_2_, bf16[512,512]{1,0:T(8,128)(2,1)S(1)} %collective-permute-done.4.refs_3_, ...), custom_call_target="tpu_custom_call" | custom-call | bytes 8388608 | tf_op jit(solution)/shard_map/pallas_call | solution.py:79
  24.4 2.3 %shard_map.105.refs_2_ = bf16[2048,2048]{1,0:T(8,128)(2,1)} custom-call(bf16[2048,512]{1,0:T(8,128)(2,1)S(1)} %shard_map.104.refs_0_, bf16[2048,512]{1,0:T(8,128)(2,1)S(1)} %collective-permute-done.2.refs_1_), custom_call_target="tpu_custom_call" | custom-call | bytes 8388608 | tf_op jit(solution)/shard_map/pallas_call | solution.py:79
  26.7 30.7 %collective-permute-done.1.train_ref = bf16[512,2048]{1,0:T(8,128)(2,1)S(1)} collective-permute-done((bf16[512,2048]{1,0:T(8,128)(2,1)}, bf16[512,2048]{1,0:T(8,128)(2,1)S(1)}, u32[]{:S(2)}, u32[]{:S(2)}) %collective-permute-start.1) | collective-permute-done | bytes 2097184 | tf_op jit(solution)/shard_map/ppermute | solution.py:98
  57.5 0.2 collective-permute-done.9.low_ref
  57.6 1.5 %shard_map.113.refs_0_ = bf16[1024,512]{1,0:T(8,128)(2,1)S(1)} custom-call(bf16[512,2048]{1,0:T(8,128)(2,1)S(1)} %collective-permute-done.1.train_ref, bf16[16,512]{1,0:T(8,128)(2,1)S(1)} %collective-permute-done.9.low_ref, bf16[16,2048]{1,0:T(8,128)(2,1)S(1)} %copy-done.4), custom_call_target="tpu_custom_call" | custom-call | flops 16777216 | bytes 2097152 | tf_op jit(solution)/shard_map/pallas_call | solution.py:34
  59.1 0.1 collective-permute-start.11
  59.2 1.5 %shard_map.112.refs_0_ = bf16[1024,512]{1,0:T(8,128)(2,1)S(1)} custom-call(bf16[512,2048]{1,0:T(8,128)(2,1)S(1)} %collective-permute-done.1.train_ref, bf16[16,512]{1,0:T(8,128)(2,1)S(1)} %collective-permute-done.9.low_ref, bf16[16,2048]{1,0:T(8,128)(2,1)S(1)} %copy-done.4), custom_call_target="tpu_custom_call" | custom-call | flops 16777216 | bytes 2097152 | tf_op jit(solution)/shard_map/pallas_call | solution.py:34
  60.7 0.6 collective-permute-start.10
  61.3 1.7 %collective-permute-start = (bf16[768,512]{1,0:T(8,128)(2,1)S(1)}, bf16[768,512]{1,0:T(8,128)(2,1)S(1)}, u32[]{:S(2)}, u32[]{:S(2)}) collective-permute-start(bf16[768,512]{1,0:T(8,128)(2,1)S(1)} %shard_map.103.refs_0_), channel_id=1, source_target_pairs={{0,8},{4,12},{8,0},{12,4},{1,9},{5,13},{9,1},{13,5},{2,10},{6,14},... | collective-permute-start | bytes 2359304 | tf_op jit(solution)/shard_map/ppermute | solution.py:98
  63.0 1.5 %shard_map.114.refs_2_ = bf16[2048,2048]{1,0:T(8,128)(2,1)} custom-call(bf16[1024,512]{1,0:T(8,128)(2,1)S(1)} %shard_map.113.refs_0_, bf16[1024,512]{1,0:T(8,128)(2,1)S(1)} %collective-permute-done.11.refs_1_, bf16[2048,2048]{1,0:T(8,128)(2,1)} %shard_map.105.refs_2_), custom_call_target="tpu_custom_call", output_to_operand_aliasing={{}: (2, {})} | custom-call | bytes 4194304 | tf_op jit(solution)/shard_map/pallas_call | solution.py:79
  64.5 1.5 %shard_map.115 = bf16[2048,2048]{1,0:T(8,128)(2,1)} custom-call(bf16[1024,512]{1,0:T(8,128)(2,1)S(1)} %shard_map.112.refs_0_, bf16[1024,512]{1,0:T(8,128)(2,1)S(1)} %collective-permute-done.10.refs_1_, bf16[2048,2048]{1,0:T(8,128)(2,1)} %shard_map.114.refs_2_), custom_call_target="tpu_custom_call", output_to_operand_aliasing={{}: (2, {})} | custom-call | bytes 4194304 | tf_op jit(solution)/shard_map/pallas_call | solution.py:79
  66.0 14.8 %collective-permute-done.refs_0_ = bf16[768,512]{1,0:T(8,128)(2,1)S(1)} collective-permute-done((bf16[768,512]{1,0:T(8,128)(2,1)S(1)}, bf16[768,512]{1,0:T(8,128)(2,1)S(1)}, u32[]{:S(2)}, u32[]{:S(2)}) %collective-permute-start) | collective-permute-done | bytes 786464 | tf_op jit(solution)/shard_map/ppermute | solution.py:98
  80.8 1.7 %collective-permute-start.16 = (bf16[512,512]{1,0:T(8,128)(2,1)S(1)}, bf16[512,512]{1,0:T(8,128)(2,1)S(1)}, u32[]{:S(2)}, u32[]{:S(2)}) collective-permute-start(bf16[512,512]{1,0:T(8,128)(2,1)S(1)} %shard_map.106.refs_2_), channel_id=1, source_target_pairs={{0,8},{4,12},{8,0},{12,4},{1,9},{5,13},{9,1},{13,5},{2,10},{6,14},... | collective-permute-start | bytes 1572872 | tf_op jit(solution)/shard_map/ppermute | solution.py:98
  82.5 0.5 collective-permute-done.17.refs_1_
  83.1 1.3 %shard_map.116.refs_2_ = bf16[2048,2048]{1,0:T(8,128)(2,1)} custom-call(bf16[768,512]{1,0:T(8,128)(2,1)S(1)} %collective-permute-done.refs_0_, bf16[768,512]{1,0:T(8,128)(2,1)S(1)} %collective-permute-done.17.refs_1_, bf16[2048,2048]{1,0:T(8,128)(2,1)} %shard_map.111.refs_2_), custom_call_target="tpu_custom_call", output_to_operand_aliasing={{}: (2, {})} | custom-call | bytes 3145728 | tf_op jit(solution)/shard_map/pallas_call | solution.py:79
  84.4 10.8 %collective-permute-done.16.refs_0_ = bf16[512,512]{1,0:T(8,128)(2,1)S(1)} collective-permute-done((bf16[512,512]{1,0:T(8,128)(2,1)S(1)}, bf16[512,512]{1,0:T(8,128)(2,1)S(1)}, u32[]{:S(2)}, u32[]{:S(2)}) %collective-permute-start.16) | collective-permute-done | bytes 524320 | tf_op jit(solution)/shard_map/ppermute | solution.py:98
  95.1 1.7 %collective-permute-start.15 = (bf16[256,512]{1,0:T(8,128)(2,1)S(1)}, bf16[256,512]{1,0:T(8,128)(2,1)S(1)}, u32[]{:S(2)}, u32[]{:S(2)}) collective-permute-start(bf16[256,512]{1,0:T(8,128)(2,1)S(1)} %shard_map.107.refs_4_), channel_id=1, source_target_pairs={{0,8},{4,12},{8,0},{12,4},{1,9},{5,13},{9,1},{13,5},{2,10},{6,14},... | collective-permute-start | bytes 786440 | tf_op jit(solution)/shard_map/ppermute | solution.py:98
  96.9 0.3 collective-permute-start.14
  97.2 1.1 shard_map.117.refs_2_
  98.2 6.1 %collective-permute-done.15.refs_0_ = bf16[256,512]{1,0:T(8,128)(2,1)S(1)} collective-permute-done((bf16[256,512]{1,0:T(8,128)(2,1)S(1)}, bf16[256,512]{1,0:T(8,128)(2,1)S(1)}, u32[]{:S(2)}, u32[]{:S(2)}) %collective-permute-start.15) | collective-permute-done | bytes 262176 | tf_op jit(solution)/shard_map/ppermute | solution.py:98
  104.4 1.5 %collective-permute-done.19.refs_1_ = bf16[256,512]{1,0:T(8,128)(2,1)S(1)} collective-permute-done((bf16[256,512]{1,0:T(8,128)(2,1)S(1)}, bf16[256,512]{1,0:T(8,128)(2,1)S(1)}, u32[]{:S(2)}, u32[]{:S(2)}) %collective-permute-start.19) | collective-permute-done | bytes 262176 | tf_op jit(solution)/shard_map/ppermute | solution.py:98
  105.8 0.9 shard_map.118.refs_2_
  106.7 2.8 %collective-permute-done.14.refs_0_ = bf16[256,512]{1,0:T(8,128)(2,1)S(1)} collective-permute-done((bf16[256,512]{1,0:T(8,128)(2,1)S(1)}, bf16[256,512]{1,0:T(8,128)(2,1)S(1)}, u32[]{:S(2)}, u32[]{:S(2)}) %collective-permute-start.14) | collective-permute-done | bytes 262176 | tf_op jit(solution)/shard_map/ppermute | solution.py:98
  109.5 0.1 broadcast_select_fusion
  109.5 1.8 %collective-permute-start.23 = (bf16[16,128]{1,0:T(8,128)(2,1)S(1)}, bf16[16,128]{1,0:T(8,128)(2,1)S(1)}, u32[]{:S(2)}, u32[]{:S(2)}) collective-permute-start(bf16[16,128]{1,0:T(8,128)(2,1)S(1)} %broadcast_select_fusion), channel_id=1, source_target_pairs={{0,1},{1,0},{2,3},{3,2},{4,5},{5,4},{6,7},{7,6},{8,9},{9,8},{10,11... | collective-permute-start | bytes 12296 | tf_op jit(solution)/shard_map/ppermute | solution.py:98
  111.3 1.5 %collective-permute-start.13 = (bf16[128,512]{1,0:T(8,128)(2,1)S(1)}, bf16[128,512]{1,0:T(8,128)(2,1)S(1)}, u32[]{:S(2)}, u32[]{:S(2)}) collective-permute-start(bf16[128,512]{1,0:T(8,128)(2,1)S(1)} %shard_map.109.refs_8_), channel_id=1, source_target_pairs={{0,8},{4,12},{8,0},{12,4},{1,9},{5,13},{9,1},{13,5},{2,10},{6,14},... | collective-permute-start | bytes 393224 | tf_op jit(solution)/shard_map/ppermute | solution.py:98
  112.9 0.3 collective-permute-done.23
  113.2 0.1 fusion
  113.2 2.8 %collective-permute-start.24 = (bf16[16,128]{1,0:T(8,128)(2,1)S(1)}, bf16[16,128]{1,0:T(8,128)(2,1)S(1)}, u32[]{:S(2)}, u32[]{:S(2)}) collective-permute-start(bf16[16,128]{1,0:T(8,128)(2,1)S(1)} %fusion), channel_id=1, source_target_pairs={{0,2},{1,3},{2,0},{3,1},{4,6},{5,7},{6,4},{7,5},{8,10},{9,11},{10,... | collective-permute-start | bytes 12296 | tf_op jit(solution)/shard_map/ppermute | solution.py:98
  116.0 1.5 %collective-permute-start.12 = (bf16[128,512]{1,0:T(8,128)(2,1)S(1)}, bf16[128,512]{1,0:T(8,128)(2,1)S(1)}, u32[]{:S(2)}, u32[]{:S(2)}) collective-permute-start(bf16[128,512]{1,0:T(8,128)(2,1)S(1)} %shard_map.110.refs_10_), channel_id=1, source_target_pairs={{0,8},{4,12},{8,0},{12,4},{1,9},{5,13},{9,1},{13,5},{2,10},{6,14},... | collective-permute-start | bytes 393224 | tf_op jit(solution)/shard_map/ppermute | solution.py:98
  117.6 0.9 shard_map.119.refs_2_
  118.4 0.1 collective-permute-start.21
  118.5 0.1 fusion.1
  118.6 0.5 collective-permute-start.25
  119.1 0.8 collective-permute-done.25
  119.9 0.8 collective-permute-start.26
  120.7 1.0 shard_map.120.refs_2_
  121.8 0.1 collective-permute-start.22
  121.9 1.7 %collective-permute-done.26 = bf16[16,128]{1,0:T(8,128)(2,1)S(1)} collective-permute-done((bf16[16,128]{1,0:T(8,128)(2,1)S(1)}, bf16[16,128]{1,0:T(8,128)(2,1)S(1)}, u32[]{:S(2)}, u32[]{:S(2)}) %collective-permute-start.26) | collective-permute-done | bytes 4128 | tf_op jit(solution)/shard_map/ppermute | solution.py:98
  123.5 0.6 add_bitcast_fusion
  124.1 1.0 shard_map.121
  (34 shorter events, 0.1 us)
Async XLA Ops:
  0.6 0.8 copy-start.3
  1.5 0.7 copy-start.5
  2.2 18.8 %copy-start.6 = (bf16[512,16]{0,1:T(8,128)(2,1)S(1)}, bf16[512,16]{0,1:T(8,128)(2,1)}, u32[]{:S(2)}) copy-start(bf16[512,16]{0,1:T(8,128)(2,1)} %param.9) | copy-start | bytes 49156
  7.7 16.7 %collective-permute-start.2 = (bf16[2048,512]{1,0:T(8,128)(2,1)S(1)}, bf16[2048,512]{1,0:T(8,128)(2,1)S(1)}, u32[]{:S(2)}, u32[]{:S(2)}) collective-permute-start(bf16[2048,512]{1,0:T(8,128)(2,1)S(1)} %shard_map.104.refs_0_), channel_id=1, source_target_pairs={{0,4},{4,0},{8,12},{12,8},{1,5},{5,1},{9,13},{13,9},{2,6},{6,2},{1... | collective-permute-start | bytes 6291464 | tf_op jit(solution)/shard_map/ppermute | solution.py:98
  8.3 49.2 %collective-permute-start.1 = (bf16[512,2048]{1,0:T(8,128)(2,1)}, bf16[512,2048]{1,0:T(8,128)(2,1)S(1)}, u32[]{:S(2)}, u32[]{:S(2)}) collective-permute-start(bf16[512,2048]{1,0:T(8,128)(2,1)} %train_ref.8), channel_id=1, source_target_pairs={{0,8},{4,12},{8,0},{12,4},{1,9},{5,13},{9,1},{13,5},{2,10},{6,14},... | collective-permute-start | bytes 6291464 | tf_op jit(solution)/shard_map/ppermute | solution.py:98
  10.9 1.6 %copy-start = (bf16[512,2048]{1,0:T(8,128)(2,1)S(1)}, bf16[512,2048]{1,0:T(8,128)(2,1)}, u32[]{:S(2)}) copy-start(bf16[512,2048]{1,0:T(8,128)(2,1)} %train_ref.13) | copy-start | bytes 6291460
  12.4 0.8 copy-start.1
  13.3 0.7 copy-start.2
  15.1 6.1 %collective-permute-start.3 = (bf16[768,512]{1,0:T(8,128)(2,1)S(1)}, bf16[768,512]{1,0:T(8,128)(2,1)S(1)}, u32[]{:S(2)}, u32[]{:S(2)}) collective-permute-start(bf16[768,512]{1,0:T(8,128)(2,1)S(1)} %shard_map.103.refs_0_), channel_id=1, source_target_pairs={{0,4},{4,0},{8,12},{12,8},{1,5},{5,1},{9,13},{13,9},{2,6},{6,2},{1... | collective-permute-start | bytes 2359304 | tf_op jit(solution)/shard_map/ppermute | solution.py:98
  15.6 2.0 %collective-permute-start.7 = (bf16[128,512]{1,0:T(8,128)(2,1)S(1)}, bf16[128,512]{1,0:T(8,128)(2,1)S(1)}, u32[]{:S(2)}, u32[]{:S(2)}) collective-permute-start(bf16[128,512]{1,0:T(8,128)(2,1)S(1)} %shard_map.109.refs_8_), channel_id=1, source_target_pairs={{0,4},{4,0},{8,12},{12,8},{1,5},{5,1},{9,13},{13,9},{2,6},{6,2},{1... | collective-permute-start | bytes 393224 | tf_op jit(solution)/shard_map/ppermute | solution.py:98
  16.3 2.2 %collective-permute-start.8 = (bf16[128,512]{1,0:T(8,128)(2,1)S(1)}, bf16[128,512]{1,0:T(8,128)(2,1)S(1)}, u32[]{:S(2)}, u32[]{:S(2)}) collective-permute-start(bf16[128,512]{1,0:T(8,128)(2,1)S(1)} %shard_map.110.refs_10_), channel_id=1, source_target_pairs={{0,4},{4,0},{8,12},{12,8},{1,5},{5,1},{9,13},{13,9},{2,6},{6,2},{1... | collective-permute-start | bytes 393224 | tf_op jit(solution)/shard_map/ppermute | solution.py:98
  17.7 1.7 %collective-permute-start.5 = (bf16[256,512]{1,0:T(8,128)(2,1)S(1)}, bf16[256,512]{1,0:T(8,128)(2,1)S(1)}, u32[]{:S(2)}, u32[]{:S(2)}) collective-permute-start(bf16[256,512]{1,0:T(8,128)(2,1)S(1)} %shard_map.107.refs_4_), channel_id=1, source_target_pairs={{0,4},{4,0},{8,12},{12,8},{1,5},{5,1},{9,13},{13,9},{2,6},{6,2},{1... | collective-permute-start | bytes 786440 | tf_op jit(solution)/shard_map/ppermute | solution.py:98
  18.6 2.6 %collective-permute-start.4 = (bf16[512,512]{1,0:T(8,128)(2,1)S(1)}, bf16[512,512]{1,0:T(8,128)(2,1)S(1)}, u32[]{:S(2)}, u32[]{:S(2)}) collective-permute-start(bf16[512,512]{1,0:T(8,128)(2,1)S(1)} %shard_map.106.refs_2_), channel_id=1, source_target_pairs={{0,4},{4,0},{8,12},{12,8},{1,5},{5,1},{9,13},{13,9},{2,6},{6,2},{1... | collective-permute-start | bytes 1572872 | tf_op jit(solution)/shard_map/ppermute | solution.py:98
  19.3 1.6 %collective-permute-start.6 = (bf16[256,512]{1,0:T(8,128)(2,1)S(1)}, bf16[256,512]{1,0:T(8,128)(2,1)S(1)}, u32[]{:S(2)}, u32[]{:S(2)}) collective-permute-start(bf16[256,512]{1,0:T(8,128)(2,1)S(1)} %shard_map.108.refs_6_), channel_id=1, source_target_pairs={{0,4},{4,0},{8,12},{12,8},{1,5},{5,1},{9,13},{13,9},{2,6},{6,2},{1... | collective-permute-start | bytes 786440 | tf_op jit(solution)/shard_map/ppermute | solution.py:98
  21.0 36.7 %collective-permute-start.9 = (bf16[16,512]{1,0:T(8,128)(2,1)S(1)}, bf16[16,512]{1,0:T(8,128)(2,1)S(1)}, u32[]{:S(2)}, u32[]{:S(2)}) collective-permute-start(bf16[16,512]{1,0:T(8,128)(2,1)S(1)} %bitcast.11), channel_id=1, source_target_pairs={{0,8},{4,12},{8,0},{12,4},{1,9},{5,13},{9,1},{13,5},{2,10},{6,14},... | collective-permute-start | bytes 49160 | tf_op jit(solution)/shard_map/ppermute | solution.py:98
  24.4 33.3 %copy-start.4 = (bf16[16,2048]{1,0:T(8,128)(2,1)S(1)}, bf16[16,2048]{1,0:T(8,128)(2,1)}, u32[]{:S(2)}) copy-start(bf16[16,2048]{1,0:T(8,128)(2,1)} %high_ref.17) | copy-start | bytes 196612
  59.1 3.9 %collective-permute-start.11 = (bf16[1024,512]{1,0:T(8,128)(2,1)S(1)}, bf16[1024,512]{1,0:T(8,128)(2,1)S(1)}, u32[]{:S(2)}, u32[]{:S(2)}) collective-permute-start(bf16[1024,512]{1,0:T(8,128)(2,1)S(1)} %shard_map.113.refs_0_), channel_id=1, source_target_pairs={{0,4},{4,0},{8,12},{12,8},{1,5},{5,1},{9,13},{13,9},{2,6},{6,2},{1... | collective-permute-start | bytes 3145736 | tf_op jit(solution)/shard_map/ppermute | solution.py:98
  60.7 3.8 %collective-permute-start.10 = (bf16[1024,512]{1,0:T(8,128)(2,1)S(1)}, bf16[1024,512]{1,0:T(8,128)(2,1)S(1)}, u32[]{:S(2)}, u32[]{:S(2)}) collective-permute-start(bf16[1024,512]{1,0:T(8,128)(2,1)S(1)} %shard_map.112.refs_0_), channel_id=1, source_target_pairs={{0,4},{4,0},{8,12},{12,8},{1,5},{5,1},{9,13},{13,9},{2,6},{6,2},{1... | collective-permute-start | bytes 3145736 | tf_op jit(solution)/shard_map/ppermute | solution.py:98
  61.3 19.5 %collective-permute-start = (bf16[768,512]{1,0:T(8,128)(2,1)S(1)}, bf16[768,512]{1,0:T(8,128)(2,1)S(1)}, u32[]{:S(2)}, u32[]{:S(2)}) collective-permute-start(bf16[768,512]{1,0:T(8,128)(2,1)S(1)} %shard_map.103.refs_0_), channel_id=1, source_target_pairs={{0,8},{4,12},{8,0},{12,4},{1,9},{5,13},{9,1},{13,5},{2,10},{6,14},... | collective-permute-start | bytes 2359304 | tf_op jit(solution)/shard_map/ppermute | solution.py:98
  80.8 2.3 %collective-permute-start.17 = (bf16[768,512]{1,0:T(8,128)(2,1)S(1)}, bf16[768,512]{1,0:T(8,128)(2,1)S(1)}, u32[]{:S(2)}, u32[]{:S(2)}) collective-permute-start(bf16[768,512]{1,0:T(8,128)(2,1)S(1)} %collective-permute-done.refs_0_), channel_id=1, source_target_pairs={{0,4},{4,0},{8,12},{12,8},{1,5},{5,1},{9,13},{13,9},{2,6},{6,2},{1... | collective-permute-start | bytes 2359304 | tf_op jit(solution)/shard_map/ppermute | solution.py:98
  80.8 14.3 %collective-permute-start.16 = (bf16[512,512]{1,0:T(8,128)(2,1)S(1)}, bf16[512,512]{1,0:T(8,128)(2,1)S(1)}, u32[]{:S(2)}, u32[]{:S(2)}) collective-permute-start(bf16[512,512]{1,0:T(8,128)(2,1)S(1)} %shard_map.106.refs_2_), channel_id=1, source_target_pairs={{0,8},{4,12},{8,0},{12,4},{1,9},{5,13},{9,1},{13,5},{2,10},{6,14},... | collective-permute-start | bytes 1572872 | tf_op jit(solution)/shard_map/ppermute | solution.py:98
  95.1 2.0 %collective-permute-start.18 = (bf16[512,512]{1,0:T(8,128)(2,1)S(1)}, bf16[512,512]{1,0:T(8,128)(2,1)S(1)}, u32[]{:S(2)}, u32[]{:S(2)}) collective-permute-start(bf16[512,512]{1,0:T(8,128)(2,1)S(1)} %collective-permute-done.16.refs_0_), channel_id=1, source_target_pairs={{0,4},{4,0},{8,12},{12,8},{1,5},{5,1},{9,13},{13,9},{2,6},{6,2},{1... | collective-permute-start | bytes 1572872 | tf_op jit(solution)/shard_map/ppermute | solution.py:98
  95.1 9.2 %collective-permute-start.15 = (bf16[256,512]{1,0:T(8,128)(2,1)S(1)}, bf16[256,512]{1,0:T(8,128)(2,1)S(1)}, u32[]{:S(2)}, u32[]{:S(2)}) collective-permute-start(bf16[256,512]{1,0:T(8,128)(2,1)S(1)} %shard_map.107.refs_4_), channel_id=1, source_target_pairs={{0,8},{4,12},{8,0},{12,4},{1,9},{5,13},{9,1},{13,5},{2,10},{6,14},... | collective-permute-start | bytes 786440 | tf_op jit(solution)/shard_map/ppermute | solution.py:98
  96.9 12.6 %collective-permute-start.14 = (bf16[256,512]{1,0:T(8,128)(2,1)S(1)}, bf16[256,512]{1,0:T(8,128)(2,1)S(1)}, u32[]{:S(2)}, u32[]{:S(2)}) collective-permute-start(bf16[256,512]{1,0:T(8,128)(2,1)S(1)} %shard_map.108.refs_6_), channel_id=1, source_target_pairs={{0,8},{4,12},{8,0},{12,4},{1,9},{5,13},{9,1},{13,5},{2,10},{6,14},... | collective-permute-start | bytes 786440 | tf_op jit(solution)/shard_map/ppermute | solution.py:98
  97.2 7.2 %copy-start.7 = (f32[128]{0:T(128)S(1)}, f32[128]{0:T(128)}, u32[]{:S(2)}) copy-start(f32[128]{0:T(128)} %param.14) | copy-start | bytes 1540
  97.2 7.2 %copy-start.8 = (f32[128]{0:T(128)S(1)}, f32[128]{0:T(128)}, u32[]{:S(2)}) copy-start(f32[128]{0:T(128)} %param.15) | copy-start | bytes 1540
  104.3 1.5 %collective-permute-start.19 = (bf16[256,512]{1,0:T(8,128)(2,1)S(1)}, bf16[256,512]{1,0:T(8,128)(2,1)S(1)}, u32[]{:S(2)}, u32[]{:S(2)}) collective-permute-start(bf16[256,512]{1,0:T(8,128)(2,1)S(1)} %collective-permute-done.15.refs_0_), channel_id=1, source_target_pairs={{0,4},{4,0},{8,12},{12,8},{1,5},{5,1},{9,13},{13,9},{2,6},{6,2},{1... | collective-permute-start | bytes 786440 | tf_op jit(solution)/shard_map/ppermute | solution.py:98
  109.5 8.1 %collective-permute-start.20 = (bf16[256,512]{1,0:T(8,128)(2,1)S(1)}, bf16[256,512]{1,0:T(8,128)(2,1)S(1)}, u32[]{:S(2)}, u32[]{:S(2)}) collective-permute-start(bf16[256,512]{1,0:T(8,128)(2,1)S(1)} %collective-permute-done.14.refs_0_), channel_id=1, source_target_pairs={{0,4},{4,0},{8,12},{12,8},{1,5},{5,1},{9,13},{13,9},{2,6},{6,2},{1... | collective-permute-start | bytes 786440 | tf_op jit(solution)/shard_map/ppermute | solution.py:98
  109.5 3.6 %collective-permute-start.23 = (bf16[16,128]{1,0:T(8,128)(2,1)S(1)}, bf16[16,128]{1,0:T(8,128)(2,1)S(1)}, u32[]{:S(2)}, u32[]{:S(2)}) collective-permute-start(bf16[16,128]{1,0:T(8,128)(2,1)S(1)} %broadcast_select_fusion), channel_id=1, source_target_pairs={{0,1},{1,0},{2,3},{3,2},{4,5},{5,4},{6,7},{7,6},{8,9},{9,8},{10,11... | collective-permute-start | bytes 12296 | tf_op jit(solution)/shard_map/ppermute | solution.py:98
  111.3 7.1 %collective-permute-start.13 = (bf16[128,512]{1,0:T(8,128)(2,1)S(1)}, bf16[128,512]{1,0:T(8,128)(2,1)S(1)}, u32[]{:S(2)}, u32[]{:S(2)}) collective-permute-start(bf16[128,512]{1,0:T(8,128)(2,1)S(1)} %shard_map.109.refs_8_), channel_id=1, source_target_pairs={{0,8},{4,12},{8,0},{12,4},{1,9},{5,13},{9,1},{13,5},{2,10},{6,14},... | collective-permute-start | bytes 393224 | tf_op jit(solution)/shard_map/ppermute | solution.py:98
  113.2 5.3 %collective-permute-start.24 = (bf16[16,128]{1,0:T(8,128)(2,1)S(1)}, bf16[16,128]{1,0:T(8,128)(2,1)S(1)}, u32[]{:S(2)}, u32[]{:S(2)}) collective-permute-start(bf16[16,128]{1,0:T(8,128)(2,1)S(1)} %fusion), channel_id=1, source_target_pairs={{0,2},{1,3},{2,0},{3,1},{4,6},{5,7},{6,4},{7,5},{8,10},{9,11},{10,... | collective-permute-start | bytes 12296 | tf_op jit(solution)/shard_map/ppermute | solution.py:98
  116.0 5.8 %collective-permute-start.12 = (bf16[128,512]{1,0:T(8,128)(2,1)S(1)}, bf16[128,512]{1,0:T(8,128)(2,1)S(1)}, u32[]{:S(2)}, u32[]{:S(2)}) collective-permute-start(bf16[128,512]{1,0:T(8,128)(2,1)S(1)} %shard_map.110.refs_10_), channel_id=1, source_target_pairs={{0,8},{4,12},{8,0},{12,4},{1,9},{5,13},{9,1},{13,5},{2,10},{6,14},... | collective-permute-start | bytes 393224 | tf_op jit(solution)/shard_map/ppermute | solution.py:98
  118.4 2.3 %collective-permute-start.21 = (bf16[128,512]{1,0:T(8,128)(2,1)S(1)}, bf16[128,512]{1,0:T(8,128)(2,1)S(1)}, u32[]{:S(2)}, u32[]{:S(2)}) collective-permute-start(bf16[128,512]{1,0:T(8,128)(2,1)S(1)} %collective-permute-done.13.refs_0_), channel_id=1, source_target_pairs={{0,4},{4,0},{8,12},{12,8},{1,5},{5,1},{9,13},{13,9},{2,6},{6,2},{1... | collective-permute-start | bytes 393224 | tf_op jit(solution)/shard_map/ppermute | solution.py:98
  118.6 1.3 %collective-permute-start.25 = (bf16[16,128]{1,0:T(8,128)(2,1)S(1)}, bf16[16,128]{1,0:T(8,128)(2,1)S(1)}, u32[]{:S(2)}, u32[]{:S(2)}) collective-permute-start(bf16[16,128]{1,0:T(8,128)(2,1)S(1)} %fusion.1), channel_id=1, source_target_pairs={{0,4},{4,0},{8,12},{12,8},{1,5},{5,1},{9,13},{13,9},{2,6},{6,2},{1... | collective-permute-start | bytes 12296 | tf_op jit(solution)/shard_map/ppermute | solution.py:98
  119.9 3.6 %collective-permute-start.26 = (bf16[16,128]{1,0:T(8,128)(2,1)S(1)}, bf16[16,128]{1,0:T(8,128)(2,1)S(1)}, u32[]{:S(2)}, u32[]{:S(2)}) collective-permute-start(bf16[16,128]{1,0:T(8,128)(2,1)S(1)} %add.22), channel_id=1, source_target_pairs={{0,8},{4,12},{8,0},{12,4},{1,9},{5,13},{9,1},{13,5},{2,10},{6,14},... | collective-permute-start | bytes 12296 | tf_op jit(solution)/shard_map/ppermute | solution.py:98
  121.8 2.3 %collective-permute-start.22 = (bf16[128,512]{1,0:T(8,128)(2,1)S(1)}, bf16[128,512]{1,0:T(8,128)(2,1)S(1)}, u32[]{:S(2)}, u32[]{:S(2)}) collective-permute-start(bf16[128,512]{1,0:T(8,128)(2,1)S(1)} %collective-permute-done.12.refs_0_), channel_id=1, source_target_pairs={{0,4},{4,0},{8,12},{12,8},{1,5},{5,1},{9,13},{13,9},{2,6},{6,2},{1... | collective-permute-start | bytes 393224 | tf_op jit(solution)/shard_map/ppermute | solution.py:98

commit v3 on v2

--- a/solution.py
+++ b/solution.py
@@ -11,7 +11,7 @@
 mix_rate = 2.0
 ANY = pl.BlockSpec(memory_space=pl.ANY)
 RAW_PARTS = 2
-PIECES = (6, 4, 2, 2, 1, 1)
+PIECES = (6, 4, 3, 2, 1)
 UNITS = sum(PIECES)
 GRANT = pltpu.CompilerParams(vmem_limit_bytes=12 * 2**20)
 
@@ -48,11 +48,11 @@
     )(train, low, high)
 
 
-def place_kernel(spots, started, *refs):
+def place_kernel(spots, *refs):
     count = len(spots)
     blocks = refs[:count]
-    out_ref = refs[count + started]
-    held = refs[count + started + 1 : -2]
+    out_ref = refs[count]
+    held = refs[count + 1 : -2]
     in_sem, out_sem = refs[-2:]
     me = lax.axis_index("shard")
     loads, stores = [], []
@@ -73,12 +73,43 @@
         store.wait()
 
 
-def place(whole, shape, blocks, spots):
-    started = whole is not None
+def land_kernel(spots, *refs):
+    out_ref, sem = refs[-2:]
+    me = lax.axis_index("shard")
+    stores = []
+    for j, (mask, first) in enumerate(spots):
+        size, width = refs[j].shape
+        column = pl.multiple_of((me ^ mask) * width, width)
+        store = pltpu.make_async_copy(
+            refs[j], out_ref.at[pl.ds(first, size), pl.ds(column, width)], sem.at[j]
+        )
+        store.start()
+        stores.append(store)
+    for store in stores:
+        store.wait()
+
+
+def land(whole, blocks, spots):
     count = len(blocks)
     return pl.pallas_call(
-        functools.partial(place_kernel, spots, started),
-        in_specs=[ANY] * (count + started),
+        functools.partial(land_kernel, spots),
+        in_specs=[ANY] * (count + 1),
+        out_specs=ANY,
+        out_shape=jax.ShapeDtypeStruct(whole.shape, whole.dtype),
+        scratch_shapes=[pltpu.SemaphoreType.DMA((count,))],
+        input_output_aliases={count: 0},
+        compiler_params=GRANT,
+        cost_estimate=pl.CostEstimate(
+            flops=0, bytes_accessed=4 * sum(b.size for b in blocks), transcendentals=0
+        ),
+    )(*blocks, whole)
+
+
+def place(shape, blocks, spots):
+    count = len(blocks)
+    return pl.pallas_call(
+        functools.partial(place_kernel, spots),
+        in_specs=[ANY] * count,
         out_specs=ANY,
         out_shape=jax.ShapeDtypeStruct(shape, jnp.bfloat16),
         scratch_shapes=[
@@ -86,12 +117,11 @@
             pltpu.SemaphoreType.DMA((count,)),
             pltpu.SemaphoreType.DMA((count,)),
         ],
-        input_output_aliases={count: 0} if started else {},
         compiler_params=GRANT,
         cost_estimate=pl.CostEstimate(
             flops=0, bytes_accessed=4 * sum(b.size for b in blocks), transcendentals=0
         ),
-    )(*blocks, *([whole] if started else []))
+    )(*blocks)
 
 
 def swap(x, axis, size, bit):
@@ -124,27 +154,27 @@
         pieces.append((first, size, own, swap(own, "shard", n, far)))
         first += size
     held, masks = near(n, merge(train_gate, low_gate.T, high_gate, 0, inner), 0)
-    whole_gate = place(None, shape, held, tuple((m, 0) for m in masks))
+    whole_gate = place(shape, held, tuple((m, 0) for m in masks))
     blocks, spots = [], []
     for first, size, own, _ in pieces:
         held, masks = near(n, own, 0)
         blocks += held
         spots += [(m, first) for m in masks]
-    whole_up = place(None, shape, blocks, tuple(spots))
+    whole_up = place(shape, blocks, tuple(spots))
 
     raw, whole_gate, whole_up = lax.optimization_barrier((raw, whole_gate, whole_up))
     size = inner // RAW_PARTS
     for first in range(0, inner, size):
         part = merge(raw, raw_low, high_gate, first, size)
         held, masks = near(n, part, far)
-        whole_gate = place(whole_gate, shape, held, tuple((m, first) for m in masks))
+        whole_gate = land(whole_gate, held, tuple((m, first) for m in masks))
     for k, (first, size, _, part) in enumerate(pieces):
         if k:
             part, whole_up = lax.optimization_barrier((part, whole_up))
         else:
             part, whole_up, whole_gate = lax.optimization_barrier((part, whole_up, whole_gate))
         held, masks = near(n, part, far)
-        whole_up = place(whole_up, shape, held, tuple((m, first) for m in masks))
+        whole_up = land(whole_up, held, tuple((m, first) for m in masks))
     return whole_gate, whole_up
 
 

time: 126 us -> 124 us (0.984)
  starting transfers between devices: 20.3 us -> 18.9 us
    pallas_call x10 -> x9, Pallas kernels: 14.6 us -> 12.7 us  [the longest x7 7.23 us: land(): pl.pallas_call(functools.partial(land_kernel, spots), in_specs=[ANY] * (c...]
    ppermute x27 -> x24, starting transfers between devices: 20.3 us -> 18.9 us  [swap(): return lax.ppermute(x, axis, [(i, i ^ bit) for i in range(size)])]
    pallas_call x9 -> x8, Pallas kernels: 11.5 us -> 12.3 us  [merge(): pl.pallas_call(merge_kernel, grid=(size // tile,), in_specs=[pl.BlockSpec...]
    ppermute x27 -> x24, waiting for transfers between devices: 72.3 us -> 72.7 us  [swap(): return lax.ppermute(x, axis, [(i, i ^ bit) for i in range(size)])]
    unnamed x18 -> x20, local copies, waits for them, and re-layouts: 4.72 us -> 4.76 us
  transfers between devices with their start and end apart: 27 -> 24, of which waited for: 13 -> 13; matrix products, arithmetic and copies ran while one was open for 1% -> 1% of each run, Pallas kernels for 14% -> 14%
where the time goes in v3:
time: 124 us; the launch traced here: 123 us
  waiting for transfers between devices  72.7 us (59%)
  Pallas kernels  25 us (20%)
  starting transfers between devices  18.9 us (15%)
  local copies, waits for them, and re-layouts  4.76 us (4%)
    ppermute x24, waiting for transfers between devices, swap(): return lax.ppermute(x, axis, [(i, i ^ bit) for i in range(size)])  72.7 us
    ppermute x24, starting transfers between devices, swap(): return lax.ppermute(x, axis, [(i, i ^ bit) for i in range(size)])  18.9 us
    pallas_call x8, Pallas kernels, merge(): pl.pallas_call(merge_kernel, grid=(size // tile,), in_specs=[pl.BlockSpec...  12.3 us
    pallas_call x7, Pallas kernels, land(): pl.pallas_call(functools.partial(land_kernel, spots), in_specs=[ANY] * (c...  7.23 us
    pallas_call x2, Pallas kernels, place(): pl.pallas_call(functools.partial(place_kernel, spots), in_specs=[ANY] * c...  5.42 us
    unnamed x20, local copies, waits for them, and re-layouts  4.76 us
  transfers between devices with their start and end apart: 24, of which 13 were waited for; matrix products, arithmetic and copies ran while one was open for 1% of the time, Pallas kernels for 14%

profile of v3, /device:TPU:0, one launch (start us, length us, event | category | flops | bytes accessed | tf_op | source)
XLA Modules:
  0.0 123.1 jit_solution(11542934222267506262)
XLA Ops:
  0.6 0.0 copy-start.2
  0.6 0.0 copy-start.3
  0.7 0.9 copy-done.3
  1.5 0.7 copy-done.7
  2.2 5.5 %shard_map.104.refs_0_ = bf16[2048,512]{1,0:T(8,128)(2,1)S(1)} custom-call(bf16[512,2048]{1,0:T(8,128)(2,1)} %train_ref.7, bf16[16,512]{1,0:T(8,128)(2,1)S(1)} %bitcast.9, bf16[16,2048]{1,0:T(8,128)(2,1)S(1)} %copy-done.3), custom_call_target="tpu_custom_call" | custom-call | flops 33554432 | bytes 4194304 | tf_op jit(solution)/shard_map/pallas_call | solution.py:34
  7.8 0.6 collective-permute-start.2
  8.3 2.6 %collective-permute-start.1 = (bf16[512,2048]{1,0:T(8,128)(2,1)}, bf16[512,2048]{1,0:T(8,128)(2,1)S(1)}, u32[]{:S(2)}, u32[]{:S(2)}) collective-permute-start(bf16[512,2048]{1,0:T(8,128)(2,1)} %train_ref.7), channel_id=1, source_target_pairs={{0,8},{4,12},{8,0},{12,4},{1,9},{5,13},{9,1},{13,5},{2,10},{6,14},... | collective-permute-start | bytes 6291464 | tf_op jit(solution)/shard_map/ppermute | solution.py:128
  10.9 1.6 %copy-done = bf16[512,2048]{1,0:T(8,128)(2,1)S(1)} copy-done((bf16[512,2048]{1,0:T(8,128)(2,1)S(1)}, bf16[512,2048]{1,0:T(8,128)(2,1)}, u32[]{:S(2)}) %copy-start) | copy-done | bytes 2097176
  12.5 0.8 copy-done.1
  13.3 0.7 copy-done.5
  14.1 1.1 shard_map.103.refs_0_
  15.2 0.2 collective-permute-start.3
  15.4 0.7 shard_map.108.refs_6_
  16.1 0.4 collective-permute-start.6
  16.5 0.3 shard_map.109.refs_8_
  16.8 0.2 collective-permute-start.7
  17.0 0.8 shard_map.106.refs_2_
  17.8 0.4 collective-permute-done.7.refs_9_
  18.2 0.2 collective-permute-start.4
  18.4 1.0 shard_map.107.refs_4_
  19.4 0.0 collective-permute-done.6.refs_7_
  19.4 0.4 collective-permute-start.5
  19.8 1.4 %collective-permute-done.5.refs_5_ = bf16[384,512]{1,0:T(8,128)(2,1)S(1)} collective-permute-done((bf16[384,512]{1,0:T(8,128)(2,1)S(1)}, bf16[384,512]{1,0:T(8,128)(2,1)S(1)}, u32[]{:S(2)}, u32[]{:S(2)}) %collective-permute-start.5) | collective-permute-done | bytes 393248 | tf_op jit(solution)/shard_map/ppermute | solution.py:128
  21.2 0.3 collective-permute-start.8
  21.5 3.1 %shard_map.110.refs_2_ = bf16[2048,2048]{1,0:T(8,128)(2,1)} custom-call(bf16[768,512]{1,0:T(8,128)(2,1)S(1)} %shard_map.103.refs_0_, bf16[768,512]{1,0:T(8,128)(2,1)S(1)} %collective-permute-done.3.refs_1_, bf16[512,512]{1,0:T(8,128)(2,1)S(1)} %shard_map.106.refs_2_, bf16[512,512]{1,0:T(8,128)(2,1)S(1)} %collective-permute-done.4.refs_3_, ...), custom_call_target="tpu_custom_call" | custom-call | bytes 8388608 | tf_op jit(solution)/shard_map/pallas_call | solution.py:110
  24.6 0.0 copy-start.4
  24.6 2.3 %shard_map.105.refs_2_ = bf16[2048,2048]{1,0:T(8,128)(2,1)} custom-call(bf16[2048,512]{1,0:T(8,128)(2,1)S(1)} %shard_map.104.refs_0_, bf16[2048,512]{1,0:T(8,128)(2,1)S(1)} %collective-permute-done.2.refs_1_), custom_call_target="tpu_custom_call" | custom-call | bytes 8388608 | tf_op jit(solution)/shard_map/pallas_call | solution.py:110
  26.9 30.6 %collective-permute-done.1.train_ref = bf16[512,2048]{1,0:T(8,128)(2,1)S(1)} collective-permute-done((bf16[512,2048]{1,0:T(8,128)(2,1)}, bf16[512,2048]{1,0:T(8,128)(2,1)S(1)}, u32[]{:S(2)}, u32[]{:S(2)}) %collective-permute-start.1) | collective-permute-done | bytes 2097184 | tf_op jit(solution)/shard_map/ppermute | solution.py:128
  57.5 0.2 collective-permute-done.8.low_ref
  57.7 1.5 %shard_map.112.refs_0_ = bf16[1024,512]{1,0:T(8,128)(2,1)S(1)} custom-call(bf16[512,2048]{1,0:T(8,128)(2,1)S(1)} %collective-permute-done.1.train_ref, bf16[16,512]{1,0:T(8,128)(2,1)S(1)} %collective-permute-done.8.low_ref, bf16[16,2048]{1,0:T(8,128)(2,1)S(1)} %copy-done.4), custom_call_target="tpu_custom_call" | custom-call | flops 16777216 | bytes 2097152 | tf_op jit(solution)/shard_map/pallas_call | solution.py:34
  59.2 0.1 collective-permute-start.10
  59.3 1.5 %shard_map.111.refs_0_ = bf16[1024,512]{1,0:T(8,128)(2,1)S(1)} custom-call(bf16[512,2048]{1,0:T(8,128)(2,1)S(1)} %collective-permute-done.1.train_ref, bf16[16,512]{1,0:T(8,128)(2,1)S(1)} %collective-permute-done.8.low_ref, bf16[16,2048]{1,0:T(8,128)(2,1)S(1)} %copy-done.4), custom_call_target="tpu_custom_call" | custom-call | flops 16777216 | bytes 2097152 | tf_op jit(solution)/shard_map/pallas_call | solution.py:34
  60.8 0.6 collective-permute-start.9
  61.3 1.7 %collective-permute-start = (bf16[768,512]{1,0:T(8,128)(2,1)S(1)}, bf16[768,512]{1,0:T(8,128)(2,1)S(1)}, u32[]{:S(2)}, u32[]{:S(2)}) collective-permute-start(bf16[768,512]{1,0:T(8,128)(2,1)S(1)} %shard_map.103.refs_0_), channel_id=1, source_target_pairs={{0,8},{4,12},{8,0},{12,4},{1,9},{5,13},{9,1},{13,5},{2,10},{6,14},... | collective-permute-start | bytes 2359304 | tf_op jit(solution)/shard_map/ppermute | solution.py:128
  63.0 1.3 %shard_map.113.refs_2_ = bf16[2048,2048]{1,0:T(8,128)(2,1)} custom-call(bf16[1024,512]{1,0:T(8,128)(2,1)S(1)} %shard_map.112.refs_0_, bf16[1024,512]{1,0:T(8,128)(2,1)S(1)} %collective-permute-done.10.refs_1_, bf16[2048,2048]{1,0:T(8,128)(2,1)} %shard_map.105.refs_2_), custom_call_target="tpu_custom_call", output_to_operand_aliasing={{}: (2, {})} | custom-call | bytes 4194304 | tf_op jit(solution)/shard_map/pallas_call | solution.py:94
  64.4 1.3 %shard_map.114 = bf16[2048,2048]{1,0:T(8,128)(2,1)} custom-call(bf16[1024,512]{1,0:T(8,128)(2,1)S(1)} %shard_map.111.refs_0_, bf16[1024,512]{1,0:T(8,128)(2,1)S(1)} %collective-permute-done.9.refs_1_, bf16[2048,2048]{1,0:T(8,128)(2,1)} %shard_map.113.refs_2_), custom_call_target="tpu_custom_call", output_to_operand_aliasing={{}: (2, {})} | custom-call | bytes 4194304 | tf_op jit(solution)/shard_map/pallas_call | solution.py:94
  65.8 15.1 %collective-permute-done.refs_0_ = bf16[768,512]{1,0:T(8,128)(2,1)S(1)} collective-permute-done((bf16[768,512]{1,0:T(8,128)(2,1)S(1)}, bf16[768,512]{1,0:T(8,128)(2,1)S(1)}, u32[]{:S(2)}, u32[]{:S(2)}) %collective-permute-start) | collective-permute-done | bytes 786464 | tf_op jit(solution)/shard_map/ppermute | solution.py:128
  80.8 1.7 %collective-permute-start.14 = (bf16[512,512]{1,0:T(8,128)(2,1)S(1)}, bf16[512,512]{1,0:T(8,128)(2,1)S(1)}, u32[]{:S(2)}, u32[]{:S(2)}) collective-permute-start(bf16[512,512]{1,0:T(8,128)(2,1)S(1)} %shard_map.106.refs_2_), channel_id=1, source_target_pairs={{0,8},{4,12},{8,0},{12,4},{1,9},{5,13},{9,1},{13,5},{2,10},{6,14},... | collective-permute-start | bytes 1572872 | tf_op jit(solution)/shard_map/ppermute | solution.py:128
  82.6 0.5 collective-permute-done.15.refs_1_
  83.1 1.2 shard_map.115.refs_2_
  84.3 0.0 copy-start.8
  84.3 0.0 copy-start.9
  84.3 10.9 %collective-permute-done.14.refs_0_ = bf16[512,512]{1,0:T(8,128)(2,1)S(1)} collective-permute-done((bf16[512,512]{1,0:T(8,128)(2,1)S(1)}, bf16[512,512]{1,0:T(8,128)(2,1)S(1)}, u32[]{:S(2)}, u32[]{:S(2)}) %collective-permute-start.14) | collective-permute-done | bytes 524320 | tf_op jit(solution)/shard_map/ppermute | solution.py:128
  95.2 1.7 %collective-permute-start.13 = (bf16[384,512]{1,0:T(8,128)(2,1)S(1)}, bf16[384,512]{1,0:T(8,128)(2,1)S(1)}, u32[]{:S(2)}, u32[]{:S(2)}) collective-permute-start(bf16[384,512]{1,0:T(8,128)(2,1)S(1)} %shard_map.107.refs_4_), channel_id=1, source_target_pairs={{0,8},{4,12},{8,0},{12,4},{1,9},{5,13},{9,1},{13,5},{2,10},{6,14},... | collective-permute-start | bytes 1179656 | tf_op jit(solution)/shard_map/ppermute | solution.py:128
  96.9 0.3 collective-permute-start.12
  97.2 1.0 shard_map.116.refs_2_
  98.2 9.0 %collective-permute-done.13.refs_0_ = bf16[384,512]{1,0:T(8,128)(2,1)S(1)} collective-permute-done((bf16[384,512]{1,0:T(8,128)(2,1)S(1)}, bf16[384,512]{1,0:T(8,128)(2,1)S(1)}, u32[]{:S(2)}, u32[]{:S(2)}) %collective-permute-start.13) | collective-permute-done | bytes 393248 | tf_op jit(solution)/shard_map/ppermute | solution.py:128
  107.2 0.1 broadcast_select_fusion
  107.3 1.8 %collective-permute-start.20 = (bf16[16,128]{1,0:T(8,128)(2,1)S(1)}, bf16[16,128]{1,0:T(8,128)(2,1)S(1)}, u32[]{:S(2)}, u32[]{:S(2)}) collective-permute-start(bf16[16,128]{1,0:T(8,128)(2,1)S(1)} %broadcast_select_fusion), channel_id=1, source_target_pairs={{0,1},{1,0},{2,3},{3,2},{4,5},{5,4},{6,7},{7,6},{8,9},{9,8},{10,11... | collective-permute-start | bytes 12296 | tf_op jit(solution)/shard_map/ppermute | solution.py:128
  109.1 0.9 shard_map.117.refs_2_
  110.0 2.3 %collective-permute-done.12.refs_0_ = bf16[256,512]{1,0:T(8,128)(2,1)S(1)} collective-permute-done((bf16[256,512]{1,0:T(8,128)(2,1)S(1)}, bf16[256,512]{1,0:T(8,128)(2,1)S(1)}, u32[]{:S(2)}, u32[]{:S(2)}) %collective-permute-start.12) | collective-permute-done | bytes 262176 | tf_op jit(solution)/shard_map/ppermute | solution.py:128
  112.3 0.1 fusion
  112.4 2.8 %collective-permute-start.21 = (bf16[16,128]{1,0:T(8,128)(2,1)S(1)}, bf16[16,128]{1,0:T(8,128)(2,1)S(1)}, u32[]{:S(2)}, u32[]{:S(2)}) collective-permute-start(bf16[16,128]{1,0:T(8,128)(2,1)S(1)} %fusion), channel_id=1, source_target_pairs={{0,2},{1,3},{2,0},{3,1},{4,6},{5,7},{6,4},{7,5},{8,10},{9,11},{10,... | collective-permute-start | bytes 12296 | tf_op jit(solution)/shard_map/ppermute | solution.py:128
  115.2 1.5 %collective-permute-start.11 = (bf16[128,512]{1,0:T(8,128)(2,1)S(1)}, bf16[128,512]{1,0:T(8,128)(2,1)S(1)}, u32[]{:S(2)}, u32[]{:S(2)}) collective-permute-start(bf16[128,512]{1,0:T(8,128)(2,1)S(1)} %shard_map.109.refs_8_), channel_id=1, source_target_pairs={{0,8},{4,12},{8,0},{12,4},{1,9},{5,13},{9,1},{13,5},{2,10},{6,14},... | collective-permute-start | bytes 393224 | tf_op jit(solution)/shard_map/ppermute | solution.py:128
  116.7 0.2 collective-permute-done.21
  116.9 0.1 fusion.1
  117.0 0.0 collective-permute-start.22
  117.0 1.2 collective-permute-done.22
  118.2 1.7 %collective-permute-start.23 = (bf16[16,128]{1,0:T(8,128)(2,1)S(1)}, bf16[16,128]{1,0:T(8,128)(2,1)S(1)}, u32[]{:S(2)}, u32[]{:S(2)}) collective-permute-start(bf16[16,128]{1,0:T(8,128)(2,1)S(1)} %add.22), channel_id=1, source_target_pairs={{0,8},{4,12},{8,0},{12,4},{1,9},{5,13},{9,1},{13,5},{2,10},{6,14},... | collective-permute-start | bytes 12296 | tf_op jit(solution)/shard_map/ppermute | solution.py:128
  119.9 0.8 shard_map.118.refs_2_
  120.7 0.1 collective-permute-done.11.refs_0_
  120.8 0.9 collective-permute-done.23
  121.8 0.6 add_bitcast_fusion
  122.4 0.7 shard_map.119
  (28 shorter events, 0.1 us)
Async XLA Ops:
  0.6 16.4 %copy-start.2 = (bf16[16,2048]{1,0:T(8,128)(2,1)S(1)}, bf16[16,2048]{1,0:T(8,128)(2,1)}, u32[]{:S(2)}) copy-start(bf16[16,2048]{1,0:T(8,128)(2,1)} %high_ref.13) | copy-start | bytes 196612
  0.6 0.9 copy-start.3
  1.5 0.7 copy-start.7
  2.2 14.8 %copy-start.6 = (bf16[512,16]{0,1:T(8,128)(2,1)S(1)}, bf16[512,16]{0,1:T(8,128)(2,1)}, u32[]{:S(2)}) copy-start(bf16[512,16]{0,1:T(8,128)(2,1)} %param.12) | copy-start | bytes 49156
  7.8 16.8 %collective-permute-start.2 = (bf16[2048,512]{1,0:T(8,128)(2,1)S(1)}, bf16[2048,512]{1,0:T(8,128)(2,1)S(1)}, u32[]{:S(2)}, u32[]{:S(2)}) collective-permute-start(bf16[2048,512]{1,0:T(8,128)(2,1)S(1)} %shard_map.104.refs_0_), channel_id=1, source_target_pairs={{0,4},{4,0},{8,12},{12,8},{1,5},{5,1},{9,13},{13,9},{2,6},{6,2},{1... | collective-permute-start | bytes 6291464 | tf_op jit(solution)/shard_map/ppermute | solution.py:128
  8.3 49.2 %collective-permute-start.1 = (bf16[512,2048]{1,0:T(8,128)(2,1)}, bf16[512,2048]{1,0:T(8,128)(2,1)S(1)}, u32[]{:S(2)}, u32[]{:S(2)}) collective-permute-start(bf16[512,2048]{1,0:T(8,128)(2,1)} %train_ref.7), channel_id=1, source_target_pairs={{0,8},{4,12},{8,0},{12,4},{1,9},{5,13},{9,1},{13,5},{2,10},{6,14},... | collective-permute-start | bytes 6291464 | tf_op jit(solution)/shard_map/ppermute | solution.py:128
  10.9 1.6 %copy-start = (bf16[512,2048]{1,0:T(8,128)(2,1)S(1)}, bf16[512,2048]{1,0:T(8,128)(2,1)}, u32[]{:S(2)}) copy-start(bf16[512,2048]{1,0:T(8,128)(2,1)} %train_ref.11) | copy-start | bytes 6291460
  12.5 0.8 copy-start.1
  13.3 0.7 copy-start.5
  15.2 6.3 %collective-permute-start.3 = (bf16[768,512]{1,0:T(8,128)(2,1)S(1)}, bf16[768,512]{1,0:T(8,128)(2,1)S(1)}, u32[]{:S(2)}, u32[]{:S(2)}) collective-permute-start(bf16[768,512]{1,0:T(8,128)(2,1)S(1)} %shard_map.103.refs_0_), channel_id=1, source_target_pairs={{0,4},{4,0},{8,12},{12,8},{1,5},{5,1},{9,13},{13,9},{2,6},{6,2},{1... | collective-permute-start | bytes 2359304 | tf_op jit(solution)/shard_map/ppermute | solution.py:128
  16.1 3.3 %collective-permute-start.6 = (bf16[256,512]{1,0:T(8,128)(2,1)S(1)}, bf16[256,512]{1,0:T(8,128)(2,1)S(1)}, u32[]{:S(2)}, u32[]{:S(2)}) collective-permute-start(bf16[256,512]{1,0:T(8,128)(2,1)S(1)} %shard_map.108.refs_6_), channel_id=1, source_target_pairs={{0,4},{4,0},{8,12},{12,8},{1,5},{5,1},{9,13},{13,9},{2,6},{6,2},{1... | collective-permute-start | bytes 786440 | tf_op jit(solution)/shard_map/ppermute | solution.py:128
  16.8 1.4 %collective-permute-start.7 = (bf16[128,512]{1,0:T(8,128)(2,1)S(1)}, bf16[128,512]{1,0:T(8,128)(2,1)S(1)}, u32[]{:S(2)}, u32[]{:S(2)}) collective-permute-start(bf16[128,512]{1,0:T(8,128)(2,1)S(1)} %shard_map.109.refs_8_), channel_id=1, source_target_pairs={{0,4},{4,0},{8,12},{12,8},{1,5},{5,1},{9,13},{13,9},{2,6},{6,2},{1... | collective-permute-start | bytes 393224 | tf_op jit(solution)/shard_map/ppermute | solution.py:128
  18.2 3.3 %collective-permute-start.4 = (bf16[512,512]{1,0:T(8,128)(2,1)S(1)}, bf16[512,512]{1,0:T(8,128)(2,1)S(1)}, u32[]{:S(2)}, u32[]{:S(2)}) collective-permute-start(bf16[512,512]{1,0:T(8,128)(2,1)S(1)} %shard_map.106.refs_2_), channel_id=1, source_target_pairs={{0,4},{4,0},{8,12},{12,8},{1,5},{5,1},{9,13},{13,9},{2,6},{6,2},{1... | collective-permute-start | bytes 1572872 | tf_op jit(solution)/shard_map/ppermute | solution.py:128
  19.4 1.8 %collective-permute-start.5 = (bf16[384,512]{1,0:T(8,128)(2,1)S(1)}, bf16[384,512]{1,0:T(8,128)(2,1)S(1)}, u32[]{:S(2)}, u32[]{:S(2)}) collective-permute-start(bf16[384,512]{1,0:T(8,128)(2,1)S(1)} %shard_map.107.refs_4_), channel_id=1, source_target_pairs={{0,4},{4,0},{8,12},{12,8},{1,5},{5,1},{9,13},{13,9},{2,6},{6,2},{1... | collective-permute-start | bytes 1179656 | tf_op jit(solution)/shard_map/ppermute | solution.py:128
  21.2 36.5 %collective-permute-start.8 = (bf16[16,512]{1,0:T(8,128)(2,1)S(1)}, bf16[16,512]{1,0:T(8,128)(2,1)S(1)}, u32[]{:S(2)}, u32[]{:S(2)}) collective-permute-start(bf16[16,512]{1,0:T(8,128)(2,1)S(1)} %bitcast.10), channel_id=1, source_target_pairs={{0,8},{4,12},{8,0},{12,4},{1,9},{5,13},{9,1},{13,5},{2,10},{6,14},... | collective-permute-start | bytes 49160 | tf_op jit(solution)/shard_map/ppermute | solution.py:128
  24.6 33.1 %copy-start.4 = (bf16[16,2048]{1,0:T(8,128)(2,1)S(1)}, bf16[16,2048]{1,0:T(8,128)(2,1)}, u32[]{:S(2)}) copy-start(bf16[16,2048]{1,0:T(8,128)(2,1)} %high_ref.15) | copy-start | bytes 196612
  59.2 3.9 %collective-permute-start.10 = (bf16[1024,512]{1,0:T(8,128)(2,1)S(1)}, bf16[1024,512]{1,0:T(8,128)(2,1)S(1)}, u32[]{:S(2)}, u32[]{:S(2)}) collective-permute-start(bf16[1024,512]{1,0:T(8,128)(2,1)S(1)} %shard_map.112.refs_0_), channel_id=1, source_target_pairs={{0,4},{4,0},{8,12},{12,8},{1,5},{5,1},{9,13},{13,9},{2,6},{6,2},{1... | collective-permute-start | bytes 3145736 | tf_op jit(solution)/shard_map/ppermute | solution.py:128
  60.8 3.6 %collective-permute-start.9 = (bf16[1024,512]{1,0:T(8,128)(2,1)S(1)}, bf16[1024,512]{1,0:T(8,128)(2,1)S(1)}, u32[]{:S(2)}, u32[]{:S(2)}) collective-permute-start(bf16[1024,512]{1,0:T(8,128)(2,1)S(1)} %shard_map.111.refs_0_), channel_id=1, source_target_pairs={{0,4},{4,0},{8,12},{12,8},{1,5},{5,1},{9,13},{13,9},{2,6},{6,2},{1... | collective-permute-start | bytes 3145736 | tf_op jit(solution)/shard_map/ppermute | solution.py:128
  61.3 19.5 %collective-permute-start = (bf16[768,512]{1,0:T(8,128)(2,1)S(1)}, bf16[768,512]{1,0:T(8,128)(2,1)S(1)}, u32[]{:S(2)}, u32[]{:S(2)}) collective-permute-start(bf16[768,512]{1,0:T(8,128)(2,1)S(1)} %shard_map.103.refs_0_), channel_id=1, source_target_pairs={{0,8},{4,12},{8,0},{12,4},{1,9},{5,13},{9,1},{13,5},{2,10},{6,14},... | collective-permute-start | bytes 2359304 | tf_op jit(solution)/shard_map/ppermute | solution.py:128
  80.8 2.3 %collective-permute-start.15 = (bf16[768,512]{1,0:T(8,128)(2,1)S(1)}, bf16[768,512]{1,0:T(8,128)(2,1)S(1)}, u32[]{:S(2)}, u32[]{:S(2)}) collective-permute-start(bf16[768,512]{1,0:T(8,128)(2,1)S(1)} %collective-permute-done.refs_0_), channel_id=1, source_target_pairs={{0,4},{4,0},{8,12},{12,8},{1,5},{5,1},{9,13},{13,9},{2,6},{6,2},{1... | collective-permute-start | bytes 2359304 | tf_op jit(solution)/shard_map/ppermute | solution.py:128
  80.8 14.3 %collective-permute-start.14 = (bf16[512,512]{1,0:T(8,128)(2,1)S(1)}, bf16[512,512]{1,0:T(8,128)(2,1)S(1)}, u32[]{:S(2)}, u32[]{:S(2)}) collective-permute-start(bf16[512,512]{1,0:T(8,128)(2,1)S(1)} %shard_map.106.refs_2_), channel_id=1, source_target_pairs={{0,8},{4,12},{8,0},{12,4},{1,9},{5,13},{9,1},{13,5},{2,10},{6,14},... | collective-permute-start | bytes 1572872 | tf_op jit(solution)/shard_map/ppermute | solution.py:128
  84.3 22.9 %copy-start.8 = (f32[128]{0:T(128)S(1)}, f32[128]{0:T(128)}, u32[]{:S(2)}) copy-start(f32[128]{0:T(128)} %param.14) | copy-start | bytes 1540
  84.3 22.9 %copy-start.9 = (f32[128]{0:T(128)S(1)}, f32[128]{0:T(128)}, u32[]{:S(2)}) copy-start(f32[128]{0:T(128)} %param.15) | copy-start | bytes 1540
  95.2 2.0 %collective-permute-start.16 = (bf16[512,512]{1,0:T(8,128)(2,1)S(1)}, bf16[512,512]{1,0:T(8,128)(2,1)S(1)}, u32[]{:S(2)}, u32[]{:S(2)}) collective-permute-start(bf16[512,512]{1,0:T(8,128)(2,1)S(1)} %collective-permute-done.14.refs_0_), channel_id=1, source_target_pairs={{0,4},{4,0},{8,12},{12,8},{1,5},{5,1},{9,13},{13,9},{2,6},{6,2},{1... | collective-permute-start | bytes 1572872 | tf_op jit(solution)/shard_map/ppermute | solution.py:128
  95.2 12.0 %collective-permute-start.13 = (bf16[384,512]{1,0:T(8,128)(2,1)S(1)}, bf16[384,512]{1,0:T(8,128)(2,1)S(1)}, u32[]{:S(2)}, u32[]{:S(2)}) collective-permute-start(bf16[384,512]{1,0:T(8,128)(2,1)S(1)} %shard_map.107.refs_4_), channel_id=1, source_target_pairs={{0,8},{4,12},{8,0},{12,4},{1,9},{5,13},{9,1},{13,5},{2,10},{6,14},... | collective-permute-start | bytes 1179656 | tf_op jit(solution)/shard_map/ppermute | solution.py:128
  96.9 15.4 %collective-permute-start.12 = (bf16[256,512]{1,0:T(8,128)(2,1)S(1)}, bf16[256,512]{1,0:T(8,128)(2,1)S(1)}, u32[]{:S(2)}, u32[]{:S(2)}) collective-permute-start(bf16[256,512]{1,0:T(8,128)(2,1)S(1)} %shard_map.108.refs_6_), channel_id=1, source_target_pairs={{0,8},{4,12},{8,0},{12,4},{1,9},{5,13},{9,1},{13,5},{2,10},{6,14},... | collective-permute-start | bytes 786440 | tf_op jit(solution)/shard_map/ppermute | solution.py:128
  107.2 1.9 %collective-permute-start.17 = (bf16[384,512]{1,0:T(8,128)(2,1)S(1)}, bf16[384,512]{1,0:T(8,128)(2,1)S(1)}, u32[]{:S(2)}, u32[]{:S(2)}) collective-permute-start(bf16[384,512]{1,0:T(8,128)(2,1)S(1)} %collective-permute-done.13.refs_0_), channel_id=1, source_target_pairs={{0,4},{4,0},{8,12},{12,8},{1,5},{5,1},{9,13},{13,9},{2,6},{6,2},{1... | collective-permute-start | bytes 1179656 | tf_op jit(solution)/shard_map/ppermute | solution.py:128
  107.3 5.0 %collective-permute-start.20 = (bf16[16,128]{1,0:T(8,128)(2,1)S(1)}, bf16[16,128]{1,0:T(8,128)(2,1)S(1)}, u32[]{:S(2)}, u32[]{:S(2)}) collective-permute-start(bf16[16,128]{1,0:T(8,128)(2,1)S(1)} %broadcast_select_fusion), channel_id=1, source_target_pairs={{0,1},{1,0},{2,3},{3,2},{4,5},{5,4},{6,7},{7,6},{8,9},{9,8},{10,11... | collective-permute-start | bytes 12296 | tf_op jit(solution)/shard_map/ppermute | solution.py:128
  112.3 7.6 %collective-permute-start.18 = (bf16[256,512]{1,0:T(8,128)(2,1)S(1)}, bf16[256,512]{1,0:T(8,128)(2,1)S(1)}, u32[]{:S(2)}, u32[]{:S(2)}) collective-permute-start(bf16[256,512]{1,0:T(8,128)(2,1)S(1)} %collective-permute-done.12.refs_0_), channel_id=1, source_target_pairs={{0,4},{4,0},{8,12},{12,8},{1,5},{5,1},{9,13},{13,9},{2,6},{6,2},{1... | collective-permute-start | bytes 786440 | tf_op jit(solution)/shard_map/ppermute | solution.py:128
  112.4 4.5 %collective-permute-start.21 = (bf16[16,128]{1,0:T(8,128)(2,1)S(1)}, bf16[16,128]{1,0:T(8,128)(2,1)S(1)}, u32[]{:S(2)}, u32[]{:S(2)}) collective-permute-start(bf16[16,128]{1,0:T(8,128)(2,1)S(1)} %fusion), channel_id=1, source_target_pairs={{0,2},{1,3},{2,0},{3,1},{4,6},{5,7},{6,4},{7,5},{8,10},{9,11},{10,... | collective-permute-start | bytes 12296 | tf_op jit(solution)/shard_map/ppermute | solution.py:128
  115.2 5.6 %collective-permute-start.11 = (bf16[128,512]{1,0:T(8,128)(2,1)S(1)}, bf16[128,512]{1,0:T(8,128)(2,1)S(1)}, u32[]{:S(2)}, u32[]{:S(2)}) collective-permute-start(bf16[128,512]{1,0:T(8,128)(2,1)S(1)} %shard_map.109.refs_8_), channel_id=1, source_target_pairs={{0,8},{4,12},{8,0},{12,4},{1,9},{5,13},{9,1},{13,5},{2,10},{6,14},... | collective-permute-start | bytes 393224 | tf_op jit(solution)/shard_map/ppermute | solution.py:128
  117.0 1.2 collective-permute-start.22
  118.2 3.6 %collective-permute-start.23 = (bf16[16,128]{1,0:T(8,128)(2,1)S(1)}, bf16[16,128]{1,0:T(8,128)(2,1)S(1)}, u32[]{:S(2)}, u32[]{:S(2)}) collective-permute-start(bf16[16,128]{1,0:T(8,128)(2,1)S(1)} %add.22), channel_id=1, source_target_pairs={{0,8},{4,12},{8,0},{12,4},{1,9},{5,13},{9,1},{13,5},{2,10},{6,14},... | collective-permute-start | bytes 12296 | tf_op jit(solution)/shard_map/ppermute | solution.py:128
  120.8 1.5 %collective-permute-start.19 = (bf16[128,512]{1,0:T(8,128)(2,1)S(1)}, bf16[128,512]{1,0:T(8,128)(2,1)S(1)}, u32[]{:S(2)}, u32[]{:S(2)}) collective-permute-start(bf16[128,512]{1,0:T(8,128)(2,1)S(1)} %collective-permute-done.11.refs_0_), channel_id=1, source_target_pairs={{0,4},{4,0},{8,12},{12,8},{1,5},{5,1},{9,13},{13,9},{2,6},{6,2},{1... | collective-permute-start | bytes 393224 | tf_op jit(solution)/shard_map/ppermute | solution.py:128
